TPU v7x, 32 devices: a whole 2x2x4 slice. The times are simulated.
32 devices in a mesh: gx: 4 (over y, core), gy: 2 (over x), gz: 4 (over z).
Axes of the slice: x: 2, y: 2, z: 4, core: 2. Of those that a mesh axis runs over, the one named last changes fastest.
Arguments:
- euler_state: float32 [5, 16, 16, 512], P(None, 'gx', 'gy', 'gz'), as said below
- gravity_state: float32 [4, 16, 16, 512], P(None, 'gx', 'gy', 'gz'), may hold values from -6 to 6
Outputs:
- section_rate: float32 [5, 16, 16, 512], P(None, 'gx', 'gy', 'gz')
- gravity_next: float32 [4, 16, 16, 512], P(None, 'gx', 'gy', 'gz')
- gravity_source: float32 [4, 16, 16, 512], P(None, 'gx', 'gy', 'gz')
- residual_norm: float32 [], replicated
Inputs may be any that keep to these rules, and one draw needn't show every extreme that they name: `euler_state`: each node's density lies between 0.7 and 3.9 and its pressure, for a ratio of specific heats of 1.4, between 0.7 and 71.
All inputs are finite; a program needn't handle non-finite values.
Results may differ from a plain program's by a relative error of at most 0.0003.
Values sent between devices are 32-bit elements; how exact they have to be, the bound alone decides.
A program may use at most 64 MiB of HBM per device.

v0:
```python
import math

import jax
import jax.numpy as jnp
import numpy as np
from jax import lax
from jax.sharding import PartitionSpec as P

ITERS = 3


gamma_gas = 1.4
elem_width = 1.0
cfl_euler = 0.5
alpha_most = 0.5
indicator_level = 0.5 * 10.0 ** (-1.8 * 4.0**0.25)
indicator_slope = math.log((1.0 - 0.0001) / 0.0001) / indicator_level
coupling = 10.0
relax_time = 1.0
grav_speed = 1.0
pseudo_step = 0.3 * elem_width / 7.0


def passed_along(value, axis, by):
    size = lax.axis_size(axis)
    return lax.ppermute(value, axis, [(i, (i + by) % size) for i in range(size)])


def padded_2(cells, sides, width):
    for axis, dim in sides:
        count = lax.axis_size(axis)
        head = lax.slice_in_dim(cells, 0, width, axis=dim)
        tail = lax.slice_in_dim(cells, cells.shape[dim] - width, cells.shape[dim], axis=dim)
        cells = jnp.concatenate(
            [
                lax.ppermute(tail, axis, [(i, (i + 1) % count) for i in range(count)]),
                cells,
                lax.ppermute(head, axis, [((i + 1) % count, i) for i in range(count)]),
            ],
            axis=dim,
        )
    return cells


def lgl_tables():
    points = np.array([-1.0, -1.0 / math.sqrt(5.0), 1.0 / math.sqrt(5.0), 1.0])
    weights = np.array([1.0, 5.0, 5.0, 1.0]) / 6.0
    barycentric = np.array(
        [
            1.0
            / np.prod([points[node_a] - points[node_b] for node_b in range(4) if node_b != node_a])
            for node_a in range(4)
        ]
    )
    derivative = np.zeros((4, 4))
    for node_a in range(4):
        for node_b in range(4):
            if node_b != node_a:
                derivative[node_a, node_b] = (
                    barycentric[node_b] / barycentric[node_a] / (points[node_a] - points[node_b])
                )
        derivative[node_a, node_a] = -np.sum(derivative[node_a])
    legendre = np.stack(
        [np.ones(4), points, 0.5 * (3.0 * points**2 - 1.0), 0.5 * (5.0 * points**3 - 3.0 * points)],
        axis=1,
    )
    legendre = legendre * np.sqrt((2.0 * np.arange(4) + 1.0) / 2.0)
    gram = np.sum(weights[:, None] * legendre * legendre, axis=0)
    modal_map = (legendre * weights[:, None]).T / gram[:, None]
    return (weights, derivative, modal_map)


def diagonal_of(derivative):
    return [derivative[node_at, node_at] for node_at in range(4)]


def along(values, length, axis_pos, array_rank):
    shape_list = [1] * array_rank
    shape_list[axis_pos] = length
    return jnp.asarray(
        np.tile(np.asarray([float(item) for item in values]), length // 4).reshape(shape_list)
    )


def log_mean(left, right):
    ratio_sq = ((left - right) / (left + right)) ** 2
    is_close = ratio_sq < 0.0001
    series = (left + right) / (
        2.0 + ratio_sq * (2.0 / 3.0 + ratio_sq * (2.0 / 5.0 + ratio_sq * 2.0 / 7.0))
    )
    top_part = jnp.where(is_close, 1.0, right - left)
    low_part = jnp.where(is_close, 1.0, jnp.log(right / left))
    return jnp.where(is_close, series, top_part / low_part)


def describe(conserved, direction):
    density = conserved[0]
    velocity = conserved[1:4] / density
    pressure = (gamma_gas - 1.0) * (conserved[4] - 0.5 * jnp.sum(conserved[1:4] * velocity, axis=0))
    normal_vel = velocity[direction]
    momentum_flux = [
        conserved[1 + comp] * normal_vel + (pressure if comp == direction else 0.0)
        for comp in range(3)
    ]
    energy_flux = (conserved[4] + pressure) * normal_vel
    sound = jnp.sqrt(gamma_gas * pressure / density)
    return jnp.stack(
        [
            conserved[0],
            conserved[1],
            conserved[2],
            conserved[3],
            conserved[4],
            velocity[0],
            velocity[1],
            velocity[2],
            pressure,
            conserved[1 + direction],
        ]
        + momentum_flux
        + [energy_flux, jnp.abs(normal_vel) + sound]
    )


def euler_interface(left, right):
    speed = jnp.maximum(left[14], right[14])
    return 0.5 * (left[9:14] + right[9:14]) - 0.5 * speed * (right[0:5] - left[0:5])


def two_point(left, right, direction):
    rho_mean = log_mean(left[0], right[0])
    inv_mean = left[8] * right[8] / log_mean(left[0] * right[8], right[0] * left[8])
    vel_avg = 0.5 * (left[5:8] + right[5:8])
    pres_avg = 0.5 * (left[8] + right[8])
    vel_product = 0.5 * jnp.sum(left[5:8] * right[5:8], axis=0)
    mass_flux = rho_mean * vel_avg[direction]
    momentum = [
        mass_flux * vel_avg[comp] + (pres_avg if comp == direction else 0.0) for comp in range(3)
    ]
    energy = mass_flux * (vel_product + inv_mean / (gamma_gas - 1.0)) + 0.5 * (
        left[8] * right[5 + direction] + right[8] * left[5 + direction]
    )
    return jnp.stack([mass_flux] + momentum + [energy])


def euler_direction(described, low_desc, high_desc, direction):
    weights, derivative, modal_map = lgl_tables()
    axis_pos = direction + 1
    length = described.shape[axis_pos]
    array_rank = described.ndim
    prev_desc = jnp.concatenate(
        [low_desc, lax.slice_in_dim(described, 0, length - 1, axis=axis_pos)], axis=axis_pos
    )
    face_flux = euler_interface(prev_desc, described)
    last_face = euler_interface(
        lax.slice_in_dim(described, length - 1, length, axis=axis_pos), high_desc
    )
    next_faces = jnp.concatenate(
        [lax.slice_in_dim(face_flux, 1, length, axis=axis_pos), last_face], axis=axis_pos
    )
    own_flux = described[9:14]
    volume = (
        along([2.0 * item for item in diagonal_of(derivative)], length, axis_pos, array_rank)
        * own_flux
    )
    for offset in range(1, 4):
        partner = jnp.roll(described, -offset, axis=axis_pos)
        pair_flux = two_point(described, partner, direction)
        upward = [
            2.0 * derivative[node_at, node_at + offset] if node_at + offset < 4 else 0.0
            for node_at in range(4)
        ]
        downward = [
            2.0 * derivative[node_at, node_at - offset] if node_at - offset >= 0 else 0.0
            for node_at in range(4)
        ]
        volume = (
            volume
            + along(upward, length, axis_pos, array_rank) * pair_flux
            + along(downward, length, axis_pos, array_rank)
            * jnp.roll(pair_flux, offset, axis=axis_pos)
        )
    first_coef = along([-1.0 / weights[0], 0.0, 0.0, 0.0], length, axis_pos, array_rank)
    last_coef = along([0.0, 0.0, 0.0, 1.0 / weights[3]], length, axis_pos, array_rank)
    dg_part = volume + first_coef * (face_flux - own_flux) + last_coef * (next_faces - own_flux)
    fv_part = along(1.0 / weights, length, axis_pos, array_rank) * (next_faces - face_flux)
    return (dg_part, fv_part)


def section_rate_from(euler_state, gravity_state, low_states, high_states, alpha):
    dg_total = 0.0
    fv_total = 0.0
    speed_total = 0.0
    for direction in range(3):
        described = describe(euler_state, direction)
        dg_part, fv_part = euler_direction(
            described,
            describe(low_states[direction], direction),
            describe(high_states[direction], direction),
            direction,
        )
        dg_total = dg_total + dg_part
        fv_total = fv_total + fv_part
        speed_total = speed_total + described[14]
    grav_grad = gravity_state[1:4]
    source = jnp.concatenate(
        [
            jnp.zeros_like(euler_state[0:1]),
            -euler_state[0:1] * grav_grad,
            -jnp.sum(euler_state[1:4] * grav_grad, axis=0, keepdims=True),
        ],
        axis=0,
    )
    rate = -(2.0 / elem_width) * ((1.0 - alpha) * dg_total + alpha * fv_total) + source
    return (rate, speed_total)


def gravity_flux(gravity, direction):
    zero_field = jnp.zeros_like(gravity[0])
    parts = [-gravity[1 + direction]]
    for comp in range(3):
        parts.append(-gravity[0] / relax_time if comp == direction else zero_field)
    return jnp.stack(parts)


def gravity_interface(left, right, direction):
    return 0.5 * (
        gravity_flux(left, direction) + gravity_flux(right, direction)
    ) - 0.5 * grav_speed * (right - left)


def gravity_direction(gravity, first_face, end_face, direction):
    weights, derivative, modal_map = lgl_tables()
    axis_pos = direction + 1
    length = gravity.shape[axis_pos]
    array_rank = gravity.ndim
    own_flux = gravity_flux(gravity, direction)
    inner = gravity_interface(jnp.roll(gravity, 1, axis=axis_pos), gravity, direction)
    face_flux = jnp.concatenate(
        [first_face, lax.slice_in_dim(inner, 1, length, axis=axis_pos)], axis=axis_pos
    )
    next_faces = jnp.concatenate(
        [lax.slice_in_dim(face_flux, 1, length, axis=axis_pos), end_face], axis=axis_pos
    )
    volume = along(diagonal_of(derivative), length, axis_pos, array_rank) * own_flux
    for offset in range(1, 4):
        upward = [
            derivative[node_at, node_at + offset] if node_at + offset < 4 else 0.0
            for node_at in range(4)
        ]
        downward = [
            derivative[node_at, node_at - offset] if node_at - offset >= 0 else 0.0
            for node_at in range(4)
        ]
        volume = (
            volume
            + along(upward, length, axis_pos, array_rank)
            * jnp.roll(own_flux, -offset, axis=axis_pos)
            + along(downward, length, axis_pos, array_rank)
            * jnp.roll(own_flux, offset, axis=axis_pos)
        )
    first_coef = along([-1.0 / weights[0], 0.0, 0.0, 0.0], length, axis_pos, array_rank)
    last_coef = along([0.0, 0.0, 0.0, 1.0 / weights[3]], length, axis_pos, array_rank)
    return volume + first_coef * (face_flux - own_flux) + last_coef * (next_faces - own_flux)


def gravity_rate(gravity, first_faces, end_faces, density, density_mean):
    total = 0.0
    for direction in range(3):
        total = total + gravity_direction(
            gravity, first_faces[direction], end_faces[direction], direction
        )
    rate = -(2.0 / elem_width) * total
    rate_phi = rate[0:1] - coupling * (density[None] - density_mean)
    rate_grad = rate[1:4] - gravity[1:4] / relax_time
    return jnp.concatenate([rate_phi, rate_grad], axis=0)


def node_weights(grid_shape):
    weights, derivative, modal_map = lgl_tables()
    return (
        along(weights, grid_shape[0], 0, 3)
        * along(weights, grid_shape[1], 1, 3)
        * along(weights, grid_shape[2], 2, 3)
    )


def weighted_total(field):
    return jnp.sum(node_weights(field.shape) * field)


def element_alpha(euler_state):
    weights, derivative, modal_map = lgl_tables()
    density = euler_state[0]
    velocity = euler_state[1:4] / density
    pressure = (gamma_gas - 1.0) * (
        euler_state[4] - 0.5 * jnp.sum(euler_state[1:4] * velocity, axis=0)
    )
    product = density * pressure
    size_x, size_y, size_z = product.shape
    modal_arr = jnp.asarray(modal_map)
    along_x = jnp.einsum(
        "ai,xiyz->xayz",
        modal_arr,
        product.reshape(size_x // 4, 4, size_y, size_z),
        precision=lax.Precision.HIGHEST,
    ).reshape(product.shape)
    along_y = jnp.einsum(
        "bj,xyjz->xybz",
        modal_arr,
        along_x.reshape(size_x, size_y // 4, 4, size_z),
        precision=lax.Precision.HIGHEST,
    ).reshape(product.shape)
    block_modal = jnp.asarray(np.kron(np.eye(size_z // 4), modal_map.T))
    coeffs = jnp.dot(along_y, block_modal, precision=lax.Precision.HIGHEST)
    energy = coeffs * coeffs
    low_index = [1.0, 1.0, 1.0, 0.0]
    low_mask = (
        along(low_index, size_x, 0, 3)
        * along(low_index, size_y, 1, 3)
        * along(low_index, size_z, 2, 3)
    )
    stacked = jnp.stack([energy, energy * (1.0 - low_mask)])
    block_adder = jnp.asarray(np.kron(np.eye(size_z // 4), np.ones((4, 1))))
    summed_z = jnp.dot(stacked, block_adder, precision=lax.Precision.HIGHEST)
    block_sums = jnp.sum(
        summed_z.reshape(2, size_x // 4, 4, size_y // 4, 4, size_z // 4), axis=(2, 4)
    )
    high_share = block_sums[1] / block_sums[0]
    alpha = alpha_most / (1.0 + jnp.exp(-indicator_slope * (high_share - indicator_level)))
    return jnp.repeat(jnp.repeat(jnp.repeat(alpha, 4, axis=0), 4, axis=1), 4, axis=2)


def owner_faces(gravity):
    low_x = passed_along(gravity[:, -1:, :, :], "gx", 1)
    low_y = passed_along(gravity[:, :, -1:, :], "gy", 1)
    low_z = passed_along(gravity[:, :, :, -1:], "gz", 1)
    first_x = gravity_interface(low_x, gravity[:, 0:1, :, :], 0)
    first_y = gravity_interface(low_y, gravity[:, :, 0:1, :], 1)
    first_z = gravity_interface(low_z, gravity[:, :, :, 0:1], 2)
    end_x = passed_along(first_x, "gx", -1)
    end_y = passed_along(first_y, "gy", -1)
    end_z = passed_along(first_z, "gz", -1)
    return ([first_x, first_y, first_z], [end_x, end_y, end_z])


def local(euler_state, gravity_state):
    grid_shape = euler_state.shape[1:]
    weight_total = (
        8.0
        * (grid_shape[0] // 4)
        * (grid_shape[1] // 4)
        * (grid_shape[2] // 4)
        * lax.axis_size("gx")
        * lax.axis_size("gy")
        * lax.axis_size("gz")
    )
    padded = padded_2(euler_state, (("gx", 1), ("gy", 2), ("gz", 3)), 1)
    low_states = [
        padded[:, 0:1, 1:-1, 1:-1],
        padded[:, 1:-1, 0:1, 1:-1],
        padded[:, 1:-1, 1:-1, 0:1],
    ]
    high_states = [
        padded[:, -1:, 1:-1, 1:-1],
        padded[:, 1:-1, -1:, 1:-1],
        padded[:, 1:-1, 1:-1, -1:],
    ]
    alpha = element_alpha(euler_state)
    rate, speed_total = section_rate_from(
        euler_state, gravity_state, low_states, high_states, alpha
    )
    fastest = lax.pmax(jnp.max(speed_total), ("gx", "gy", "gz"))
    time_step = cfl_euler * elem_width / (7.0 * fastest)
    state_next = euler_state + time_step * rate
    density_mean = lax.psum(weighted_total(state_next[0]), ("gx", "gy", "gz")) / weight_total
    gravity = gravity_state
    rate_grav = jnp.zeros_like(gravity_state)
    for iteration in range(ITERS):
        first_faces, end_faces = owner_faces(gravity)
        rate_grav = gravity_rate(gravity, first_faces, end_faces, state_next[0], density_mean)
        gravity = gravity + pseudo_step * rate_grav
    squared_total = lax.psum(weighted_total(rate_grav[0] * rate_grav[0]), ("gx", "gy", "gz"))
    residual_norm = jnp.sqrt(squared_total / weight_total)
    grav_grad = gravity[1:4]
    gravity_source = jnp.concatenate(
        [
            -state_next[0:1] * grav_grad,
            -jnp.sum(state_next[1:4] * grav_grad, axis=0, keepdims=True),
        ],
        axis=0,
    )
    return (rate, gravity, gravity_source, residual_norm)


def solution(mesh):
    placed = (P(None, "gx", "gy", "gz"), P(None, "gx", "gy", "gz"))
    return jax.shard_map(
        local,
        mesh=mesh,
        in_specs=placed,
        out_specs=(
            P(None, "gx", "gy", "gz"),
            P(None, "gx", "gy", "gz"),
            P(None, "gx", "gy", "gz"),
            P(),
        ),
        check_vma=False,
    )
```

profile of v0, /device:TPU:0, one launch (start us, length us, event | category | flops | bytes accessed | tf_op | source)
XLA Modules:
  0.0 211.9 jit_solution(2786028733510712442)
XLA Ops:
  2.7 2.5 %collective-permute-start.8 = (f32[4,4,1,128]{3,2,1,0:T(1,128)S(1)}, f32[4,4,1,128]{3,2,1,0:T(1,128)S(1)}, u32[]{:S(2)}, u32[]{:S(2)}) collective-permute-start(f32[4,4,1,128]{3,2,1,0:T(1,128)S(1)} %slice.1803), channel_id=1, source_target_pairs={{0,4},{4,0},{1,5},{5,1},{2,6},{6,2},{3,7},{7,3},{8,12},{12,8},{9,1... | collective-permute-start | bytes 24584 | tf_op jit(solution)/shard_map/ppermute | solution.py:26
  6.1 1.6 collective-permute-start.10
  7.8 1.2 collective-permute-start.1
  12.6 2.3 %collective-permute-start.11 = (f32[4,4,8,1]{3,2,1,0:T(8,128)S(1)}, f32[4,4,8,1]{3,2,1,0:T(8,128)S(1)}, u32[]{:S(2)}, u32[]{:S(2)}) collective-permute-start(f32[4,4,8,1]{3,2,1,0:T(8,128)S(1)} %fusion.114), channel_id=1, source_target_pairs={{0,3},{1,0},{2,1},{3,2},{4,7},{5,4},{6,5},{7,6},{8,11},{9,8},{10,9... | collective-permute-start | bytes 1544 | tf_op jit(solution)/shard_map/ppermute | solution.py:26
  15.8 1.2 collective-permute-done.11
  17.0 1.7 collective-permute-done.9
  28.6 38.1 %pmax.7 = f32[]{:T(128)} all-reduce(f32[]{:T(128)} %fusion.288), channel_id=1, replica_groups=mesh['gx'=4,'gy'=2,'gz'=4] {'gx','gy','gz'}, use_global_device_ids=true, to_apply=%region_20.21 | all-reduce | flops 1 | bytes 8 | tf_op jit(solution)/shard_map/pmax | solution.py:373
  72.2 2.3 %collective-permute-start.3 = (f32[5,6,1,128]{3,2,1,0:T(1,128)S(1)}, f32[5,6,1,128]{3,2,1,0:T(1,128)S(1)}, u32[]{:S(2)}, u32[]{:S(2)}) collective-permute-start(f32[5,6,1,128]{3,2,1,0:T(1,128)S(1)} %get-tuple-element.154), channel_id=1, source_target_pairs={{4,0},{0,4},{5,1},{1,5},{6,2},{2,6},{7,3},{3,7},{12,8},{8,12},{13,... | collective-permute-start | bytes 46088 | tf_op jit(solution)/shard_map/ppermute | solution.py:38
  76.6 1.7 collective-permute-done.2
  79.2 2.1 collective-permute-start.4
  81.3 1.8 collective-permute-start.5
  85.2 3.8 %collective-permute-done.4 = f32[5,6,10,1]{3,2,1,0:T(8,128)S(1)} collective-permute-done((f32[5,6,10,1]{3,2,1,0:T(8,128)S(1)}, f32[5,6,10,1]{3,2,1,0:T(8,128)S(1)}, u32[]{:S(2)}, u32[]{:S(2)}) %collective-permute-start.4) | collective-permute-done | bytes 1232 | tf_op jit(solution)/shard_map/ppermute | solution.py:36
  89.5 2.0 collective-permute-done.5
  97.4 1.9 multiply_add_fusion
  99.9 38.4 %psum.14 = f32[]{:T(128)} all-reduce(f32[]{:T(128)} %fusion.195), channel_id=1, replica_groups=mesh['gx'=4,'gy'=2,'gz'=4] {'gx','gy','gz'}, use_global_device_ids=true, to_apply=%region_22.23 | all-reduce | flops 1 | bytes 8 | tf_op jit(solution)/shard_map/psum | solution.py:376
  139.9 2.3 %collective-permute-start.14 = (f32[4,4,1,128]{3,2,1,0:T(1,128)S(1)}, f32[4,4,1,128]{3,2,1,0:T(1,128)S(1)}, u32[]{:S(2)}, u32[]{:S(2)}) collective-permute-start(f32[4,4,1,128]{3,2,1,0:T(1,128)S(1)} %slice.2213), channel_id=1, source_target_pairs={{0,4},{4,0},{1,5},{5,1},{2,6},{6,2},{3,7},{7,3},{8,12},{12,8},{9,1... | collective-permute-start | bytes 24584 | tf_op jit(solution)/shard_map/ppermute | solution.py:26
  142.2 1.5 collective-permute-start.16
  144.1 4.9 %collective-permute-done.16 = f32[4,4,8,1]{3,2,1,0:T(8,128)S(1)} collective-permute-done((f32[4,4,8,1]{3,2,1,0:T(8,128)S(1)}, f32[4,4,8,1]{3,2,1,0:T(8,128)S(1)}, u32[]{:S(2)}, u32[]{:S(2)}) %collective-permute-start.16) | collective-permute-done | bytes 544 | tf_op jit(solution)/shard_map/ppermute | solution.py:26
  150.9 3.2 %collective-permute-done.17 = f32[4,4,8,1]{3,2,1,0:T(8,128)S(1)} collective-permute-done((f32[4,4,8,1]{3,2,1,0:T(8,128)S(1)}, f32[4,4,8,1]{3,2,1,0:T(8,128)S(1)}, u32[]{:S(2)}, u32[]{:S(2)}) %collective-permute-start.17) | collective-permute-done | bytes 544 | tf_op jit(solution)/shard_map/ppermute | solution.py:26
  156.2 1.5 collective-permute-start.20
  157.8 1.8 collective-permute-start.22
  159.8 4.0 %collective-permute-done.22 = f32[4,4,8,1]{3,2,1,0:T(8,128)S(1)} collective-permute-done((f32[4,4,8,1]{3,2,1,0:T(8,128)S(1)}, f32[4,4,8,1]{3,2,1,0:T(8,128)S(1)}, u32[]{:S(2)}, u32[]{:S(2)}) %collective-permute-start.22) | collective-permute-done | bytes 544 | tf_op jit(solution)/shard_map/ppermute | solution.py:26
  165.6 2.7 %collective-permute-done.23 = f32[4,4,8,1]{3,2,1,0:T(8,128)S(1)} collective-permute-done((f32[4,4,8,1]{3,2,1,0:T(8,128)S(1)}, f32[4,4,8,1]{3,2,1,0:T(8,128)S(1)}, u32[]{:S(2)}, u32[]{:S(2)}) %collective-permute-start.23) | collective-permute-done | bytes 544 | tf_op jit(solution)/shard_map/ppermute | solution.py:26
  170.0 39.4 %psum.15 = f32[]{:T(128)} all-reduce(f32[]{:T(128)} %get-tuple-element.39), channel_id=1, replica_groups=mesh['gx'=4,'gy'=2,'gz'=4] {'gx','gy','gz'}, use_global_device_ids=true, to_apply=%region_25.26 | all-reduce | flops 1 | bytes 8 | tf_op jit(solution)/shard_map/psum | solution.py:383
  (528 shorter events, 41.6 us)
Async XLA Ops:
  1.4 14.2 %collective-permute-start.6 = (f32[4,1,8,128]{3,2,1,0:T(8,128)S(1)}, f32[4,1,8,128]{3,2,1,0:T(8,128)S(1)}, u32[]{:S(2)}, u32[]{:S(2)}) collective-permute-start(f32[4,1,8,128]{3,2,1,0:T(8,128)S(1)} %slice.1780), channel_id=1, source_target_pairs={{0,8},{8,16},{16,24},{24,0},{1,9},{9,17},{17,25},{25,1},{2,10},{10... | collective-permute-start | bytes 49160 | tf_op jit(solution)/shard_map/ppermute | solution.py:26
  2.7 12.2 %collective-permute-start.8 = (f32[4,4,1,128]{3,2,1,0:T(1,128)S(1)}, f32[4,4,1,128]{3,2,1,0:T(1,128)S(1)}, u32[]{:S(2)}, u32[]{:S(2)}) collective-permute-start(f32[4,4,1,128]{3,2,1,0:T(1,128)S(1)} %slice.1803), channel_id=1, source_target_pairs={{0,4},{4,0},{1,5},{5,1},{2,6},{6,2},{3,7},{7,3},{8,12},{12,8},{9,1... | collective-permute-start | bytes 24584 | tf_op jit(solution)/shard_map/ppermute | solution.py:26
  6.1 6.4 %collective-permute-start.10 = (f32[4,4,8,1]{3,2,1,0:T(8,128)S(1)}, f32[4,4,8,1]{3,2,1,0:T(8,128)S(1)}, u32[]{:S(2)}, u32[]{:S(2)}) collective-permute-start(f32[4,4,8,1]{3,2,1,0:T(8,128)S(1)} %slice.1826), channel_id=1, source_target_pairs={{0,1},{1,2},{2,3},{3,0},{4,5},{5,6},{6,7},{7,4},{8,9},{9,10},{10,1... | collective-permute-start | bytes 1544 | tf_op jit(solution)/shard_map/ppermute | solution.py:26
  7.8 8.0 %collective-permute-start.1 = (f32[5,1,8,128]{3,2,1,0:T(8,128)S(1)}, f32[5,1,8,128]{3,2,1,0:T(8,128)S(1)}, u32[]{:S(2)}, u32[]{:S(2)}) collective-permute-start(f32[5,1,8,128]{3,2,1,0:T(8,128)S(1)} %slice.1642), channel_id=1, source_target_pairs={{8,0},{16,8},{24,16},{0,24},{9,1},{17,9},{25,17},{1,25},{10,2},{18... | collective-permute-start | bytes 61448 | tf_op jit(solution)/shard_map/ppermute | solution.py:38
  12.6 4.4 %collective-permute-start.11 = (f32[4,4,8,1]{3,2,1,0:T(8,128)S(1)}, f32[4,4,8,1]{3,2,1,0:T(8,128)S(1)}, u32[]{:S(2)}, u32[]{:S(2)}) collective-permute-start(f32[4,4,8,1]{3,2,1,0:T(8,128)S(1)} %fusion.114), channel_id=1, source_target_pairs={{0,3},{1,0},{2,1},{3,2},{4,7},{5,4},{6,5},{7,6},{8,11},{9,8},{10,9... | collective-permute-start | bytes 1544 | tf_op jit(solution)/shard_map/ppermute | solution.py:26
  15.0 3.7 %collective-permute-start.9 = (f32[4,4,1,128]{3,2,1,0:T(1,128)S(1)}, f32[4,4,1,128]{3,2,1,0:T(1,128)S(1)}, u32[]{:S(2)}, u32[]{:S(2)}) collective-permute-start(f32[4,4,1,128]{3,2,1,0:T(1,128)S(1)} %fusion.329), channel_id=1, source_target_pairs={{0,4},{4,0},{1,5},{5,1},{2,6},{6,2},{3,7},{7,3},{8,12},{12,8},{9,1... | collective-permute-start | bytes 24584 | tf_op jit(solution)/shard_map/ppermute | solution.py:26
  15.7 3.0 %collective-permute-start.7 = (f32[4,1,8,128]{3,2,1,0:T(8,128)S(1)}, f32[4,1,8,128]{3,2,1,0:T(8,128)S(1)}, u32[]{:S(2)}, u32[]{:S(2)}) collective-permute-start(f32[4,1,8,128]{3,2,1,0:T(8,128)S(1)} %fusion.284), channel_id=1, source_target_pairs={{0,24},{8,0},{16,8},{24,16},{1,25},{9,1},{17,9},{25,17},{2,26},{10... | collective-permute-start | bytes 49160 | tf_op jit(solution)/shard_map/ppermute | solution.py:26
  25.1 45.7 %collective-permute-start = (f32[5,1,8,128]{3,2,1,0:T(8,128)S(1)}, f32[5,1,8,128]{3,2,1,0:T(8,128)S(1)}, u32[]{:S(2)}, u32[]{:S(2)}) collective-permute-start(f32[5,1,8,128]{3,2,1,0:T(8,128)S(1)} %get-tuple-element.182), channel_id=1, source_target_pairs={{0,8},{8,16},{16,24},{24,0},{1,9},{9,17},{17,25},{25,1},{2,10},{10... | collective-permute-start | bytes 61448 | tf_op jit(solution)/shard_map/ppermute | solution.py:36
  72.2 4.3 %collective-permute-start.3 = (f32[5,6,1,128]{3,2,1,0:T(1,128)S(1)}, f32[5,6,1,128]{3,2,1,0:T(1,128)S(1)}, u32[]{:S(2)}, u32[]{:S(2)}) collective-permute-start(f32[5,6,1,128]{3,2,1,0:T(1,128)S(1)} %get-tuple-element.154), channel_id=1, source_target_pairs={{4,0},{0,4},{5,1},{1,5},{6,2},{2,6},{7,3},{3,7},{12,8},{8,12},{13,... | collective-permute-start | bytes 46088 | tf_op jit(solution)/shard_map/ppermute | solution.py:38
  74.6 3.7 %collective-permute-start.2 = (f32[5,6,1,128]{3,2,1,0:T(1,128)S(1)}, f32[5,6,1,128]{3,2,1,0:T(1,128)S(1)}, u32[]{:S(2)}, u32[]{:S(2)}) collective-permute-start(f32[5,6,1,128]{3,2,1,0:T(1,128)S(1)} %get-tuple-element.153), channel_id=1, source_target_pairs={{0,4},{4,0},{1,5},{5,1},{2,6},{6,2},{3,7},{7,3},{8,12},{12,8},{9,1... | collective-permute-start | bytes 46088 | tf_op jit(solution)/shard_map/ppermute | solution.py:36
  79.2 9.9 %collective-permute-start.4 = (f32[5,6,10,1]{3,2,1,0:T(8,128)S(1)}, f32[5,6,10,1]{3,2,1,0:T(8,128)S(1)}, u32[]{:S(2)}, u32[]{:S(2)}) collective-permute-start(f32[5,6,10,1]{3,2,1,0:T(8,128)S(1)} %get-tuple-element.122), channel_id=1, source_target_pairs={{0,1},{1,2},{2,3},{3,0},{4,5},{5,6},{6,7},{7,4},{8,9},{9,10},{10,1... | collective-permute-start | bytes 3608 | tf_op jit(solution)/shard_map/ppermute | solution.py:36
  81.3 10.3 %collective-permute-start.5 = (f32[5,6,10,1]{3,2,1,0:T(8,128)}, f32[5,6,10,1]{3,2,1,0:T(8,128)S(1)}, u32[]{:S(2)}, u32[]{:S(2)}) collective-permute-start(f32[5,6,10,1]{3,2,1,0:T(8,128)} %get-tuple-element.121), channel_id=1, source_target_pairs={{1,0},{2,1},{3,2},{0,3},{5,4},{6,5},{7,6},{4,7},{9,8},{10,9},{11,1... | collective-permute-start | bytes 3608 | tf_op jit(solution)/shard_map/ppermute | solution.py:38
  139.8 10.3 %collective-permute-start.12 = (f32[4,1,8,128]{3,2,1,0:T(8,128)S(1)}, f32[4,1,8,128]{3,2,1,0:T(8,128)S(1)}, u32[]{:S(2)}, u32[]{:S(2)}) collective-permute-start(f32[4,1,8,128]{3,2,1,0:T(8,128)S(1)} %slice.2187), channel_id=1, source_target_pairs={{0,8},{8,16},{16,24},{24,0},{1,9},{9,17},{17,25},{25,1},{2,10},{10... | collective-permute-start | bytes 49160 | tf_op jit(solution)/shard_map/ppermute | solution.py:26
  139.9 10.1 %collective-permute-start.14 = (f32[4,4,1,128]{3,2,1,0:T(1,128)S(1)}, f32[4,4,1,128]{3,2,1,0:T(1,128)S(1)}, u32[]{:S(2)}, u32[]{:S(2)}) collective-permute-start(f32[4,4,1,128]{3,2,1,0:T(1,128)S(1)} %slice.2213), channel_id=1, source_target_pairs={{0,4},{4,0},{1,5},{5,1},{2,6},{6,2},{3,7},{7,3},{8,12},{12,8},{9,1... | collective-permute-start | bytes 24584 | tf_op jit(solution)/shard_map/ppermute | solution.py:26
  142.2 6.7 %collective-permute-start.16 = (f32[4,4,8,1]{3,2,1,0:T(8,128)S(1)}, f32[4,4,8,1]{3,2,1,0:T(8,128)S(1)}, u32[]{:S(2)}, u32[]{:S(2)}) collective-permute-start(f32[4,4,8,1]{3,2,1,0:T(8,128)S(1)} %slice.2239), channel_id=1, source_target_pairs={{0,1},{1,2},{2,3},{3,0},{4,5},{5,6},{6,7},{7,4},{8,9},{9,10},{10,1... | collective-permute-start | bytes 1544 | tf_op jit(solution)/shard_map/ppermute | solution.py:26
  149.9 4.3 %collective-permute-start.17 = (f32[4,4,8,1]{3,2,1,0:T(8,128)S(1)}, f32[4,4,8,1]{3,2,1,0:T(8,128)S(1)}, u32[]{:S(2)}, u32[]{:S(2)}) collective-permute-start(f32[4,4,8,1]{3,2,1,0:T(8,128)S(1)} %fusion.84), channel_id=1, source_target_pairs={{0,3},{1,0},{2,1},{3,2},{4,7},{5,4},{6,5},{7,6},{8,11},{9,8},{10,9... | collective-permute-start | bytes 1544 | tf_op jit(solution)/shard_map/ppermute | solution.py:26
  150.0 4.2 %collective-permute-start.15 = (f32[4,4,1,128]{3,2,1,0:T(1,128)S(1)}, f32[4,4,1,128]{3,2,1,0:T(1,128)S(1)}, u32[]{:S(2)}, u32[]{:S(2)}) collective-permute-start(f32[4,4,1,128]{3,2,1,0:T(1,128)S(1)} %fusion.327), channel_id=1, source_target_pairs={{0,4},{4,0},{1,5},{5,1},{2,6},{6,2},{3,7},{7,3},{8,12},{12,8},{9,1... | collective-permute-start | bytes 24584 | tf_op jit(solution)/shard_map/ppermute | solution.py:26
  150.8 3.4 %collective-permute-start.13 = (f32[4,1,8,128]{3,2,1,0:T(8,128)S(1)}, f32[4,1,8,128]{3,2,1,0:T(8,128)S(1)}, u32[]{:S(2)}, u32[]{:S(2)}) collective-permute-start(f32[4,1,8,128]{3,2,1,0:T(8,128)S(1)} %fusion.244), channel_id=1, source_target_pairs={{0,24},{8,0},{16,8},{24,16},{1,25},{9,1},{17,9},{25,17},{2,26},{10... | collective-permute-start | bytes 49160 | tf_op jit(solution)/shard_map/ppermute | solution.py:26
  156.0 9.0 %collective-permute-start.18 = (f32[4,1,8,128]{3,2,1,0:T(8,128)S(1)}, f32[4,1,8,128]{3,2,1,0:T(8,128)S(1)}, u32[]{:S(2)}, u32[]{:S(2)}) collective-permute-start(f32[4,1,8,128]{3,2,1,0:T(8,128)S(1)} %slice.2263), channel_id=1, source_target_pairs={{0,8},{8,16},{16,24},{24,0},{1,9},{9,17},{17,25},{25,1},{2,10},{10... | collective-permute-start | bytes 49160 | tf_op jit(solution)/shard_map/ppermute | solution.py:26
  156.2 7.8 %collective-permute-start.20 = (f32[4,4,1,128]{3,2,1,0:T(1,128)S(1)}, f32[4,4,1,128]{3,2,1,0:T(1,128)S(1)}, u32[]{:S(2)}, u32[]{:S(2)}) collective-permute-start(f32[4,4,1,128]{3,2,1,0:T(1,128)S(1)} %slice.2289), channel_id=1, source_target_pairs={{0,4},{4,0},{1,5},{5,1},{2,6},{6,2},{3,7},{7,3},{8,12},{12,8},{9,1... | collective-permute-start | bytes 24584 | tf_op jit(solution)/shard_map/ppermute | solution.py:26
  157.8 6.1 %collective-permute-start.22 = (f32[4,4,8,1]{3,2,1,0:T(8,128)S(1)}, f32[4,4,8,1]{3,2,1,0:T(8,128)S(1)}, u32[]{:S(2)}, u32[]{:S(2)}) collective-permute-start(f32[4,4,8,1]{3,2,1,0:T(8,128)S(1)} %slice.2315), channel_id=1, source_target_pairs={{0,1},{1,2},{2,3},{3,0},{4,5},{5,6},{6,7},{7,4},{8,9},{9,10},{10,1... | collective-permute-start | bytes 1544 | tf_op jit(solution)/shard_map/ppermute | solution.py:26
  164.0 4.3 %collective-permute-start.23 = (f32[4,4,8,1]{3,2,1,0:T(8,128)S(1)}, f32[4,4,8,1]{3,2,1,0:T(8,128)S(1)}, u32[]{:S(2)}, u32[]{:S(2)}) collective-permute-start(f32[4,4,8,1]{3,2,1,0:T(8,128)S(1)} %fusion.80), channel_id=1, source_target_pairs={{0,3},{1,0},{2,1},{3,2},{4,7},{5,4},{6,5},{7,6},{8,11},{9,8},{10,9... | collective-permute-start | bytes 1544 | tf_op jit(solution)/shard_map/ppermute | solution.py:26
  164.1 4.2 %collective-permute-start.21 = (f32[4,4,1,128]{3,2,1,0:T(1,128)S(1)}, f32[4,4,1,128]{3,2,1,0:T(1,128)S(1)}, u32[]{:S(2)}, u32[]{:S(2)}) collective-permute-start(f32[4,4,1,128]{3,2,1,0:T(1,128)S(1)} %fusion.325), channel_id=1, source_target_pairs={{0,4},{4,0},{1,5},{5,1},{2,6},{6,2},{3,7},{7,3},{8,12},{12,8},{9,1... | collective-permute-start | bytes 24584 | tf_op jit(solution)/shard_map/ppermute | solution.py:26
  165.1 3.2 %collective-permute-start.19 = (f32[4,1,8,128]{3,2,1,0:T(8,128)S(1)}, f32[4,1,8,128]{3,2,1,0:T(8,128)S(1)}, u32[]{:S(2)}, u32[]{:S(2)}) collective-permute-start(f32[4,1,8,128]{3,2,1,0:T(8,128)S(1)} %fusion.242), channel_id=1, source_target_pairs={{0,24},{8,0},{16,8},{24,16},{1,25},{9,1},{17,9},{25,17},{2,26},{10... | collective-permute-start | bytes 49160 | tf_op jit(solution)/shard_map/ppermute | solution.py:26
  (109 other events, 202.4 us)
where the time goes:
time: 213 us; the launch traced here: 212 us
  blocking collectives  116 us (54%)
  waiting for transfers between devices  26 us (12%)
  starting transfers between devices  24.4 us (11%)
  local copies, waits for them, and re-layouts  22.8 us (11%)
  other arithmetic  16 us (8%)
  between operations  6.14 us (3%)
    psum x1, blocking collectives, local(): lax.psum(weighted_total(rate_grav[0] * rate_grav[0]), ('gx', 'gy', 'gz'))  39.4 us
    psum x1, blocking collectives, local(): lax.psum(weighted_total(state_next[0]), ('gx', 'gy', 'gz')) / weight_total  38.4 us
    pmax x1, blocking collectives, local(): fastest = lax.pmax(jnp.max(speed_total), ('gx', 'gy', 'gz'))  38.1 us
    ppermute x18, waiting for transfers between devices, passed_along(): lax.ppermute(value, axis, [(i, (i + by) % size) for i in range(size)])  18.3 us
    ppermute x18, starting transfers between devices, passed_along(): lax.ppermute(value, axis, [(i, (i + by) % size) for i in range(size)])  16.7 us
    unnamed x237, local copies, waits for them, and re-layouts  10.1 us
    ppermute x3, waiting for transfers between devices, padded_2(): lax.ppermute(tail, axis, [(i, (i + 1) % count) for i in range(count)])  5.56 us
    ppermute x3, starting transfers between devices, padded_2(): lax.ppermute(head, axis, [((i + 1) % count, i) for i in range(count)])  5.31 us
  transfers between devices with their start and end apart: 24, of which 10 were waited for; matrix products, arithmetic and copies ran while one was open for 6% of the time, Pallas kernels for 0%

commit v1 on v0

v1 whole, which is shorter than its diff:
```python
import itertools
import math

import jax
import jax.numpy as jnp
import numpy as np
from jax import lax
from jax.experimental import pallas as pl
from jax.experimental.pallas import tpu as pltpu
from jax.sharding import PartitionSpec as P

ITERS = 3
AXES = ("gx", "gy", "gz")
MOST_PARTNERS = 64

gamma_gas = 1.4
elem_width = 1.0
cfl_euler = 0.5
alpha_most = 0.5
indicator_level = 0.5 * 10.0 ** (-1.8 * 4.0**0.25)
indicator_slope = math.log((1.0 - 0.0001) / 0.0001) / indicator_level
coupling = 10.0
relax_time = 1.0
grav_speed = 1.0
pseudo_step = 0.3 * elem_width / 7.0
MESH = pl.DeviceIdType.MESH


def lgl_tables():
    points = np.array([-1.0, -1.0 / math.sqrt(5.0), 1.0 / math.sqrt(5.0), 1.0])
    weights = np.array([1.0, 5.0, 5.0, 1.0]) / 6.0
    barycentric = np.array(
        [
            1.0
            / np.prod([points[node_a] - points[node_b] for node_b in range(4) if node_b != node_a])
            for node_a in range(4)
        ]
    )
    derivative = np.zeros((4, 4))
    for node_a in range(4):
        for node_b in range(4):
            if node_b != node_a:
                derivative[node_a, node_b] = (
                    barycentric[node_b] / barycentric[node_a] / (points[node_a] - points[node_b])
                )
        derivative[node_a, node_a] = -np.sum(derivative[node_a])
    legendre = np.stack(
        [np.ones(4), points, 0.5 * (3.0 * points**2 - 1.0), 0.5 * (5.0 * points**3 - 3.0 * points)],
        axis=1,
    )
    legendre = legendre * np.sqrt((2.0 * np.arange(4) + 1.0) / 2.0)
    gram = np.sum(weights[:, None] * legendre * legendre, axis=0)
    modal_map = (legendre * weights[:, None]).T / gram[:, None]
    return (weights, derivative, modal_map)


WEIGHTS, DERIV, MODAL = lgl_tables()
DERIV_FOLDED = DERIV.copy()
DERIV_FOLDED[0, 0] += 1.0 / WEIGHTS[0]
DERIV_FOLDED[3, 3] -= 1.0 / WEIGHTS[3]
SELF_COEF = 2.0 * np.diag(DERIV)
SELF_COEF[0] += 1.0 / WEIGHTS[0]
SELF_COEF[3] -= 1.0 / WEIGHTS[3]


def reduce_stages(sizes):
    total = math.prod(sizes[axis] for axis in AXES)
    if total <= MOST_PARTNERS:
        return [AXES]
    return [("gx", "gy"), ("gz",)]


def offsets_of(axes, sizes):
    ranges = [range(sizes[axis]) for axis in axes]
    return [item for item in itertools.product(*ranges) if any(item)]


class Plane:
    def __init__(self, ny, nz):
        self.shape = (ny, nz)
        self.index = [lax.broadcasted_iota(jnp.int32, (ny, nz), axis) for axis in range(2)]
        self.node = [item & 3 for item in self.index]
        self.is_node = [[node == value for value in range(4)] for node in self.node]
        self.cache = {}

    def coef(self, values, axis):
        values = tuple(float(np.float32(value)) for value in values)
        if len(set(values)) == 1:
            return values[0]
        key = (values, axis)
        if key not in self.cache:
            result = jnp.full(self.shape, values[3], jnp.float32)
            for node in range(2, -1, -1):
                result = jnp.where(self.is_node[axis][node], values[node], result)
            self.cache[key] = result
        return self.cache[key]

    def ahead(self, value, by, axis):
        return pltpu.roll(value, (-by) % self.shape[axis], axis)

    def apply(self, matrix, value, axis):
        total = self.coef(np.diag(matrix), axis) * value
        for by in range(1, 4):
            up = [matrix[node, node + by] if node + by < 4 else 0.0 for node in range(4)]
            down = [matrix[node, node - by] if node - by >= 0 else 0.0 for node in range(4)]
            total = total + self.coef(up, axis) * self.ahead(value, by, axis)
            total = total + self.coef(down, axis) * self.ahead(value, -by, axis)
        return total

    def previous(self, value, halo, axis):
        return jnp.where(self.index[axis] == 0, halo, self.ahead(value, -1, axis))

    def following(self, value, halo, axis):
        last = self.shape[axis] - 1
        return jnp.where(self.index[axis] == last, halo, self.ahead(value, 1, axis))


def primitive(state):
    inverse = 1.0 / state[0]
    vel = [state[1 + comp] * inverse for comp in range(3)]
    kinetic = state[1] * vel[0] + state[2] * vel[1] + state[3] * vel[2]
    pressure = (gamma_gas - 1.0) * (state[4] - 0.5 * kinetic)
    sound = jnp.sqrt(gamma_gas * pressure * inverse)
    return list(state) + vel + [pressure, sound]


def flux_of(node, direction):
    normal = node[5 + direction]
    momentum = [
        node[1 + comp] * normal + node[8] if comp == direction else node[1 + comp] * normal
        for comp in range(3)
    ]
    return [node[1 + direction]] + momentum + [(node[4] + node[8]) * normal]


def euler_interface(left, right, direction):
    speed = 0.5 * jnp.maximum(
        jnp.abs(left[5 + direction]) + left[9], jnp.abs(right[5 + direction]) + right[9]
    )
    flux_left, flux_right = flux_of(left, direction), flux_of(right, direction)
    return [
        0.5 * (flux_left[var] + flux_right[var]) - speed * (right[var] - left[var])
        for var in range(5)
    ]


def log_mean_parts(left, right):
    total = left + right
    ratio = (left - right) / total
    ratio_sq = ratio * ratio
    is_close = ratio_sq < 0.0001
    series = 2.0 + ratio_sq * (2.0 / 3.0 + ratio_sq * (2.0 / 5.0 + ratio_sq * (2.0 / 7.0)))
    top = jnp.where(is_close, total, right - left)
    low = jnp.where(is_close, series, jnp.log(right / left))
    return top, low


def two_point(left, right, direction):
    top, low = log_mean_parts(left[0], right[0])
    rho_mean = top / low
    top, low = log_mean_parts(left[0] * right[4], right[0] * left[4])
    inv_mean = left[4] * right[4] * low / top
    vel_avg = [0.5 * (left[1 + comp] + right[1 + comp]) for comp in range(3)]
    pres_avg = 0.5 * (left[4] + right[4])
    vel_product = 0.5 * (left[1] * right[1] + left[2] * right[2] + left[3] * right[3])
    mass = rho_mean * vel_avg[direction]
    momentum = [
        mass * vel_avg[comp] + pres_avg if comp == direction else mass * vel_avg[comp]
        for comp in range(3)
    ]
    energy = mass * (vel_product + inv_mean * (1.0 / (gamma_gas - 1.0))) + 0.5 * (
        left[4] * right[1 + direction] + right[4] * left[1 + direction]
    )
    return [mass] + momentum + [energy]


def gravity_interface(left, right, direction):
    result = []
    for var in range(4):
        jump = 0.5 * grav_speed * (right[var] - left[var])
        if var == 0:
            result.append(-0.5 * (left[1 + direction] + right[1 + direction]) - jump)
        elif var == 1 + direction:
            result.append(-(0.5 / relax_time) * (left[0] + right[0]) - jump)
        else:
            result.append(-jump)
    return result


def add_volume(volume, nodes, plane, nx):
    pair_fields = [[node[0], node[5], node[6], node[7], node[8]] for node in nodes]

    def add(x, terms):
        for var in range(5):
            old = volume[var][x]
            volume[var][x] = terms[var] if old is None else old + terms[var]

    for start in range(0, nx, 4):
        for low in range(4):
            own = flux_of(nodes[start + low], 0)
            coef = float(np.float32(SELF_COEF[low]))
            add(start + low, [coef * item for item in own])
            for high in range(low + 1, 4):
                flux = two_point(pair_fields[start + low], pair_fields[start + high], 0)
                add(start + low, [float(2.0 * DERIV[low, high]) * item for item in flux])
                add(start + high, [float(2.0 * DERIV[high, low]) * item for item in flux])
    deriv = 2.0 * DERIV
    for axis in range(2):
        direction = axis + 1
        for x in range(nx):
            here = pair_fields[x]
            own = flux_of(nodes[x], direction)
            coef = plane.coef(SELF_COEF, axis)
            add(x, [coef * item for item in own])
            there = [plane.ahead(item, 1, axis) for item in here]
            flux = two_point(here, there, direction)
            up = plane.coef([deriv[0, 1], deriv[1, 2], deriv[2, 3], 0.0], axis)
            down = plane.coef([0.0, deriv[1, 0], deriv[2, 1], deriv[3, 2]], axis)
            add(x, [up * item + down * plane.ahead(item, -1, axis) for item in flux])
            is_last = plane.is_node[axis][3]
            there = [
                jnp.where(is_last, plane.ahead(item, -3, axis), plane.ahead(item, 2, axis))
                for item in here
            ]
            flux = two_point(here, there, direction)
            own_coef = plane.coef([deriv[0, 2], deriv[1, 3], 0.0, deriv[3, 0]], axis)
            down = plane.coef([0.0, 0.0, deriv[2, 0], deriv[3, 1]], axis)
            up = plane.coef([deriv[0, 3], 0.0, 0.0, 0.0], axis)
            add(
                x,
                [
                    own_coef * item
                    + down * plane.ahead(item, -2, axis)
                    + up * plane.ahead(item, 3, axis)
                    for item in flux
                ],
            )


def element_alpha(nodes, plane, nx):
    ones = np.ones((4, 4))
    low_index = np.array([1.0, 1.0, 1.0, 0.0])
    not_low = 1.0 - plane.coef(low_index, 0) * plane.coef(low_index, 1)
    result = []
    for start in range(0, nx, 4):
        product = [nodes[start + node][0] * nodes[start + node][8] for node in range(4)]
        energies = []
        for mode in range(4):
            coeffs = sum(float(MODAL[mode, node]) * product[node] for node in range(4))
            coeffs = plane.apply(MODAL, plane.apply(MODAL, coeffs, 0), 1)
            energies.append(coeffs * coeffs)
        low_part = energies[0] + energies[1] + energies[2]
        sums = [low_part + energies[3], low_part * not_low + energies[3]]
        sums = [plane.apply(ones, plane.apply(ones, item, 1), 0) for item in sums]
        share = sums[1] / sums[0]
        alpha = alpha_most / (1.0 + jnp.exp(-indicator_slope * (share - indicator_level)))
        result += [alpha] * 4
    return result


def make_kernel(sizes, shape):
    nx, ny, nz = shape
    stages = reduce_stages(sizes)
    weight_total = (
        8.0 * (nx // 4) * (ny // 4) * (nz // 4) * math.prod(sizes[axis] for axis in AXES)
    )

    def kernel(
        euler_hbm,
        gravity_hbm,
        rate_ref,
        grav_ref,
        source_ref,
        norm_ref,
        euler_ref,
        grav_bufs,
        halo_xe,
        halo_xg,
        send_y,
        recv_y,
        send_z,
        recv_z,
        reduce_send,
        *rest,
    ):
        reduce_recv = rest[: len(stages)]
        load_sem, send_sem, recv_sem, reduce_send_sem, reduce_recv_sem = rest[len(stages) :]
        place = {axis: lax.axis_index(axis) for axis in AXES}

        def moved(axis, by):
            size = sizes[axis]
            by = by % size
            if by == 0:
                return place[axis]
            target = place[axis] + by
            return jnp.where(target >= size, target - size, target)

        targets = {axis: [moved(axis, by) for by in range(sizes[axis])] for axis in AXES}

        def device(axes, offset):
            return {axis: targets[axis][by] for axis, by in zip(axes, offset)}

        barrier = pltpu.get_barrier_semaphore()
        count = 0
        for axes in stages:
            for offset in offsets_of(axes, sizes):
                pl.semaphore_signal(
                    barrier, inc=1, device_id=device(axes, offset), device_id_type=MESH
                )
                count += 1
        load_euler = pltpu.make_async_copy(euler_hbm, euler_ref, load_sem.at[0])
        load_gravity = pltpu.make_async_copy(gravity_hbm, grav_bufs.at[0], load_sem.at[1])
        load_euler.start()
        load_gravity.start()
        load_euler.wait()
        load_gravity.wait()

        plane = Plane(ny, nz)
        state = [[euler_ref[var, x] for x in range(nx)] for var in range(5)]
        grav = [[grav_bufs[0, var, x] for x in range(nx)] for var in range(4)]

        def pack(round_at, fields):
            lanes = [jnp.zeros((ny, nz), jnp.float32) for side in range(2)]
            for at, item in enumerate(itertools.chain(*fields)):
                send_y[round_at, 0, at : at + 1, :] = item[ny - 1 : ny, :]
                send_y[round_at, 1, at : at + 1, :] = item[0:1, :]
                here = plane.index[1] == at
                lanes[0] = jnp.where(here, plane.ahead(item, nz - 1 - at, 1), lanes[0])
                lanes[1] = jnp.where(here, plane.ahead(item, -at, 1), lanes[1])
            send_z[round_at, 0] = lanes[0]
            send_z[round_at, 1] = lanes[1]

        def exchange(round_at):
            copies = []

            def send(src, dst, slot, axis, by):
                copy = pltpu.make_async_remote_copy(
                    src_ref=src,
                    dst_ref=dst,
                    send_sem=send_sem.at[round_at, slot],
                    recv_sem=recv_sem.at[round_at, slot],
                    device_id=device((axis,), (by % sizes[axis],)),
                    device_id_type=MESH,
                )
                copy.start()
                copies.append(copy)

            for side, by in ((0, 1), (1, -1)):
                face = nx - 1 if side == 0 else 0
                if round_at == 0:
                    send(euler_ref.at[:, face], halo_xe.at[side], 6 + side, "gx", by)
                send(
                    grav_bufs.at[round_at, :, face], halo_xg.at[round_at, side], side, "gx", by
                )
                rows = recv_y.shape[2] if round_at == 0 else 8 * ((4 * nx + 7) // 8)
                send(
                    send_y.at[round_at, side, pl.ds(0, rows)],
                    recv_y.at[round_at, side, pl.ds(0, rows)],
                    2 + side,
                    "gy",
                    by,
                )
                send(send_z.at[round_at, side], recv_z.at[round_at, side], 4 + side, "gz", by)
            return copies

        def halo_y(round_at, side, at):
            return jnp.broadcast_to(recv_y[round_at, side, at : at + 1, :], (ny, nz))

        def halo_z(column, at):
            return jnp.broadcast_to(column[:, at : at + 1], (ny, nz))

        def reduce_start(round_at, stage_at, rows):
            axes = stages[stage_at]
            for at, row in enumerate(rows):
                reduce_send[round_at, stage_at, at] = row
            copies = []
            for slot, offset in enumerate(offsets_of(axes, sizes)):
                copy = pltpu.make_async_remote_copy(
                    src_ref=reduce_send.at[round_at, stage_at, pl.ds(0, len(rows))],
                    dst_ref=reduce_recv[stage_at].at[round_at, slot, pl.ds(0, len(rows))],
                    send_sem=reduce_send_sem.at[round_at, stage_at],
                    recv_sem=reduce_recv_sem.at[round_at, stage_at],
                    device_id=device(axes, offset),
                    device_id_type=MESH,
                )
                copy.start()

        def reduce_finish(round_at, rows, combine):
            for stage_at in range(len(stages)):
                if stage_at > 0:
                    reduce_start(round_at, stage_at, rows)
                got = reduce_recv[stage_at].at[round_at, :, pl.ds(0, len(rows))]
                pltpu.make_async_copy(got, got, reduce_recv_sem.at[round_at, stage_at]).wait()
                pltpu.make_async_copy(got, got, reduce_send_sem.at[round_at, stage_at]).wait()
                partners = reduce_recv[stage_at].shape[1]
                new_rows = []
                for at, row in enumerate(rows):
                    parts = [row] + [
                        reduce_recv[stage_at][round_at, slot, at] for slot in range(partners)
                    ]
                    while len(parts) > 1:
                        pairs = [
                            combine[at](parts[item], parts[item + 1])
                            for item in range(0, len(parts) - 1, 2)
                        ]
                        parts = pairs + ([parts[-1]] if len(parts) % 2 else [])
                    new_rows.append(parts[0])
                rows = new_rows
            return rows

        pack(0, state + grav)
        nodes = [primitive([state[var][x] for var in range(5)]) for x in range(nx)]
        weight_yz = plane.coef(WEIGHTS, 0) * plane.coef(WEIGHTS, 1)

        def weighted_row(items):
            total = sum(float(WEIGHTS[x % 4]) * items[x] for x in range(nx))
            return jnp.sum(weight_yz * total, axis=0, keepdims=True)

        speeds = [
            jnp.abs(node[5]) + jnp.abs(node[6]) + jnp.abs(node[7]) + 3.0 * node[9] for node in nodes
        ]
        fastest = speeds[0]
        for item in speeds[1:]:
            fastest = jnp.maximum(fastest, item)
        first_rows = [jnp.max(fastest, axis=0, keepdims=True), weighted_row(state[0])]

        pl.semaphore_wait(barrier, count)
        copies_0 = exchange(0)
        reduce_start(0, 0, first_rows)

        alpha = element_alpha(nodes, plane, nx)
        volume = [[None] * nx for var in range(5)]
        add_volume(volume, nodes, plane, nx)
        total = [[(1.0 - alpha[x]) * volume[var][x] for x in range(nx)] for var in range(5)]

        for copy in copies_0:
            copy.wait()

        def face_coefs(axis, alpha_x):
            start = jnp.where(plane.is_node[axis][0], 1.0, alpha_x)
            stop = jnp.where(plane.is_node[axis][3], 1.0, alpha_x)
            inverse = plane.coef(1.0 / WEIGHTS, axis)
            return start * inverse, stop * inverse

        edges = [primitive([halo_xe[side, var] for var in range(5)]) for side in range(2)]
        row = [edges[0]] + nodes + [edges[1]]
        faces = [euler_interface(row[at], row[at + 1], 0) for at in range(nx + 1)]
        for x in range(nx):
            node = x % 4
            start = 1.0 / WEIGHTS[0] if node == 0 else alpha[x] * float(1.0 / WEIGHTS[node])
            stop = 1.0 / WEIGHTS[3] if node == 3 else alpha[x] * float(1.0 / WEIGHTS[node])
            for var in range(5):
                total[var][x] += stop * faces[x + 1][var] - start * faces[x][var]
        column = [recv_z[0, side] for side in range(2)]
        for axis in range(2):
            for x in range(nx):
                start, stop = face_coefs(axis, alpha[x])
                halos = [
                    [
                        halo_y(0, side, var * nx + x)
                        if axis == 0
                        else halo_z(column[side], var * nx + x)
                        for var in range(5)
                    ]
                    for side in range(2)
                ]
                before = primitive(
                    [plane.previous(state[var][x], halos[0][var], axis) for var in range(5)]
                )
                after = primitive(
                    [plane.following(state[var][x], halos[1][var], axis) for var in range(5)]
                )
                left = euler_interface(before, nodes[x], axis + 1)
                right = euler_interface(nodes[x], after, axis + 1)
                for var in range(5):
                    total[var][x] += stop * right[var] - start * left[var]
        rate = [[-(2.0 / elem_width) * total[var][x] for x in range(nx)] for var in range(5)]
        for x in range(nx):
            for comp in range(3):
                rate[1 + comp][x] = rate[1 + comp][x] - state[0][x] * grav[1 + comp][x]
            rate[4][x] = rate[4][x] - (
                state[1][x] * grav[1][x] + state[2][x] * grav[2][x] + state[3][x] * grav[3][x]
            )
            for var in range(5):
                rate_ref[var, x] = rate[var][x]
        mass_rows = [weighted_row(rate[0])]
        reduce_start(1, 0, mass_rows)

        first_rows = reduce_finish(0, first_rows, [jnp.maximum, jnp.add])
        fastest = jnp.max(first_rows[0], axis=1, keepdims=True)
        mean_now = jnp.sum(first_rows[1], axis=1, keepdims=True) * (1.0 / weight_total)
        time_step = cfl_euler * elem_width / (7.0 * fastest)
        state_next = [
            [state[var][x] + time_step * rate[var][x] for x in range(nx)] for var in range(4)
        ]

        def gravity_rate(grav, round_at, offset):
            result = [
                [-coupling * (state_next[0][x] - offset) for x in range(nx)],
            ] + [[-grav[1 + comp][x] / relax_time for x in range(nx)] for comp in range(3)]
            scale = -(2.0 / elem_width)
            for start in range(0, nx, 4):
                for node in range(4):
                    for other in range(4):
                        coef = float(-scale * DERIV_FOLDED[node, other])
                        result[0][start + node] += coef * grav[1][start + other]
                        result[1][start + node] += coef / relax_time * grav[0][start + other]
            for axis in range(2):
                for x in range(nx):
                    matrix = -scale * DERIV_FOLDED
                    result[0][x] += plane.apply(matrix, grav[2 + axis][x], axis)
                    result[2 + axis][x] += plane.apply(matrix / relax_time, grav[0][x], axis)
            return result, scale

        def gravity_faces(result, scale, grav, round_at, first_at):
            edges = [[halo_xg[round_at, side, var] for var in range(4)] for side in range(2)]
            row = [edges[0]] + [[grav[var][x] for var in range(4)] for x in range(nx)] + [edges[1]]
            for x in range(0, nx, 4):
                left = gravity_interface(row[x], row[x + 1], 0)
                right = gravity_interface(row[x + 4], row[x + 5], 0)
                for var in range(4):
                    result[var][x] += float(-scale / WEIGHTS[0]) * left[var]
                    result[var][x + 3] += float(scale / WEIGHTS[3]) * right[var]
            column = [recv_z[round_at, side] for side in range(2)]
            for axis in range(2):
                start = plane.coef([-scale / WEIGHTS[0], 0.0, 0.0, 0.0], axis)
                stop = plane.coef([0.0, 0.0, 0.0, scale / WEIGHTS[3]], axis)
                for x in range(nx):
                    halos = [
                        [
                            halo_y(round_at, side, first_at + var * nx + x)
                            if axis == 0
                            else halo_z(column[side], first_at + var * nx + x)
                            for var in range(4)
                        ]
                        for side in range(2)
                    ]
                    here = [grav[var][x] for var in range(4)]
                    before = [plane.previous(here[var], halos[0][var], axis) for var in range(4)]
                    after = [plane.following(here[var], halos[1][var], axis) for var in range(4)]
                    left = gravity_interface(before, here, axis + 1)
                    right = gravity_interface(here, after, axis + 1)
                    for var in range(4):
                        result[var][x] += start * left[var] + stop * right[var]
            return result

        for iteration in range(ITERS):
            rate_grav, scale = gravity_rate(grav, iteration, mean_now)
            if iteration > 0:
                for copy in copies:
                    copy.wait()
            rate_grav = gravity_faces(
                rate_grav, scale, grav, iteration, 5 * nx if iteration == 0 else 0
            )
            if iteration < ITERS - 1:
                grav = [
                    [grav[var][x] + pseudo_step * rate_grav[var][x] for x in range(nx)]
                    for var in range(4)
                ]
                for var in range(4):
                    for x in range(nx):
                        grav_bufs[iteration + 1, var, x] = grav[var][x]
                pack(iteration + 1, grav)
                copies = exchange(iteration + 1)
        mass_rows = reduce_finish(1, mass_rows, [jnp.add])
        mean_more = time_step * (
            jnp.sum(mass_rows[0], axis=1, keepdims=True) * (1.0 / weight_total)
        )
        rate_phi = [item + coupling * mean_more for item in rate_grav[0]]
        norm_rows = [weighted_row([item * item for item in rate_phi])]
        reduce_start(2, 0, norm_rows)
        late = (ITERS - 1) * pseudo_step * coupling * mean_more
        rate_grav[0] = rate_phi
        grav = [
            [grav[var][x] + pseudo_step * rate_grav[var][x] for x in range(nx)] for var in range(4)
        ]
        for x in range(nx):
            grav[0][x] = grav[0][x] + late
            for var in range(4):
                grav_ref[var, x] = grav[var][x]
            for comp in range(3):
                source_ref[comp, x] = -state_next[0][x] * grav[1 + comp][x]
            source_ref[3, x] = -(
                state_next[1][x] * grav[1][x]
                + state_next[2][x] * grav[2][x]
                + state_next[3][x] * grav[3][x]
            )
        norm_rows = reduce_finish(2, norm_rows, [jnp.add])
        squared = jnp.sum(norm_rows[0], axis=1, keepdims=True)
        norm_ref[...] = jnp.sqrt(squared * (1.0 / weight_total))

    rows_y = 8 * ((9 * nx + 7) // 8)
    plane_shape = (ny, nz)
    scratch = [
        pltpu.VMEM((5, nx) + plane_shape, jnp.float32),
        pltpu.VMEM((ITERS, 4, nx) + plane_shape, jnp.float32),
        pltpu.VMEM((2, 5) + plane_shape, jnp.float32),
        pltpu.VMEM((ITERS, 2, 4) + plane_shape, jnp.float32),
        pltpu.VMEM((ITERS, 2, rows_y, nz), jnp.float32),
        pltpu.VMEM((ITERS, 2, rows_y, nz), jnp.float32),
        pltpu.VMEM((ITERS, 2) + plane_shape, jnp.float32),
        pltpu.VMEM((ITERS, 2) + plane_shape, jnp.float32),
        pltpu.VMEM((3, len(stages), 2, 1, nz), jnp.float32),
    ]
    for axes in stages:
        scratch.append(pltpu.VMEM((3, len(offsets_of(axes, sizes)), 2, 1, nz), jnp.float32))
    scratch += [
        pltpu.SemaphoreType.DMA((2,)),
        pltpu.SemaphoreType.DMA((ITERS, 8)),
        pltpu.SemaphoreType.DMA((ITERS, 8)),
        pltpu.SemaphoreType.DMA((3, len(stages))),
        pltpu.SemaphoreType.DMA((3, len(stages))),
    ]
    return kernel, scratch


def solution(mesh):
    sizes = {axis: mesh.shape[axis] for axis in AXES}

    def local(euler_state, gravity_state):
        shape = euler_state.shape[1:]
        kernel, scratch = make_kernel(sizes, shape)
        vmem = pl.BlockSpec(memory_space=pltpu.VMEM)
        rate, gravity, source, norm = pl.pallas_call(
            kernel,
            out_shape=(
                jax.ShapeDtypeStruct((5,) + shape, jnp.float32),
                jax.ShapeDtypeStruct((4,) + shape, jnp.float32),
                jax.ShapeDtypeStruct((4,) + shape, jnp.float32),
                jax.ShapeDtypeStruct((1, 1), jnp.float32),
            ),
            in_specs=[pl.BlockSpec(memory_space=pl.ANY)] * 2,
            out_specs=(vmem, vmem, vmem, vmem),
            scratch_shapes=scratch,
            compiler_params=pltpu.CompilerParams(collective_id=0, has_side_effects=True),
        )(euler_state, gravity_state)
        return rate, gravity, source, norm.reshape(())

    placed = (P(None, "gx", "gy", "gz"), P(None, "gx", "gy", "gz"))
    return jax.shard_map(
        local,
        mesh=mesh,
        in_specs=placed,
        out_specs=placed[:1] * 3 + (P(),),
        check_vma=False,
    )
```

time: 213 us -> 31.1 us (0.15)
  blocking collectives: 116 us -> 0 us
  waiting for transfers between devices: 26 us -> 0 us
  Pallas kernels: 0 us -> 25.4 us
  starting transfers between devices: 24.4 us -> 0 us
  local copies, waits for them, and re-layouts: 22.8 us -> 3.05 us
  other arithmetic: 16 us -> 0 us
  between operations: 6.14 us -> 2.4 us
    psum x2 -> x0, blocking collectives: 77.8 us -> none  [the longest x1 39.4 us: local(): lax.psum(weighted_total(rate_grav[0] * rate_grav[0]), ('gx', 'gy', 'gz'))]
    pmax x1 -> x0, blocking collectives: 38.1 us -> none  [local(): fastest = lax.pmax(jnp.max(speed_total), ('gx', 'gy', 'gz'))]
    ppermute x24 -> x0, waiting for transfers between devices: 26 us -> none  [the longest x18 18.3 us: passed_along(): lax.ppermute(value, axis, [(i, (i + by) % size) for i in range(size)])]
    pallas_call x0 -> x1, Pallas kernels: none -> 25.4 us  [local(): pl.pallas_call(kernel, out_shape=(jax.ShapeDtypeStruct((5,) + shape, jnp....]
    ppermute x24 -> x0, starting transfers between devices: 24.4 us -> none  [the longest x18 16.7 us: passed_along(): lax.ppermute(value, axis, [(i, (i + by) % size) for i in range(size)])]
    slice x81 -> x0, local copies, waits for them, and re-layouts: 10.3 us -> none  [the longest x11 3.93 us: euler_direction(): jnp.roll(pair_flux, offset, axis=axis_pos)]
    unnamed x237 -> x7, local copies, waits for them, and re-layouts: 10.1 us -> 3.05 us
    mul x19 -> x0, other arithmetic: 3.6 us -> none  [the longest x3 1.19 us: gravity_rate(): rate = -(2.0 / elem_width) * total]
  transfers between devices with their start and end apart: 24 -> 0, of which waited for: 10 -> 0; matrix products, arithmetic and copies ran while one was open for 6% -> 0% of each run, Pallas kernels for 0% -> 0%
where the time goes in v1:
time: 31.1 us; the launch traced here: 30.8 us
  Pallas kernels  25.4 us (82%)
  local copies, waits for them, and re-layouts  3.05 us (10%)
  between operations  2.4 us (8%)
    pallas_call x1, Pallas kernels, local(): pl.pallas_call(kernel, out_shape=(jax.ShapeDtypeStruct((5,) + shape, jnp....  25.4 us
    unnamed x7, local copies, waits for them, and re-layouts  3.05 us

profile of v1, /device:TPU:0, one launch (start us, length us, event | category | flops | bytes accessed | tf_op | source)
XLA Modules:
  0.0 30.8 jit_solution(11360998490358865969)
XLA Ops:
  0.6 25.4 %shard_map.57 = (f32[5,4,8,128]{3,2,1,0:T(8,128)}, f32[4,4,8,128]{3,2,1,0:T(8,128)}, f32[4,4,8,128]{3,2,1,0:T(8,128)}, f32[1,1]{1,0:T(1,128)}) custom-call(f32[5,4,8,128]{3,2,1,0:T(8,128)} %euler_hbm.1, f32[4,4,8,128]{3,2,1,0:T(8,128)} %gravity_hbm.1), custom_call_target="tpu_custom_call" | custom-call | tf_op jit(solution)/shard_map/pallas_call | solution.py:624
  26.0 0.0 copy-start.1
  26.0 1.6 %copy.10 = f32[5,4,8,128]{3,2,1,0:T(8,128)} copy(f32[5,4,8,128]{3,2,1,0:T(8,128)} %get-tuple-element.16) | data formatting | bytes 163840
  27.6 0.0 copy-done.1
  27.6 0.0 copy-start
  27.6 0.6 %copy.11 = f32[4,4,8,128]{3,2,1,0:T(8,128)} copy(f32[4,4,8,128]{3,2,1,0:T(8,128)S(1)} %copy-done.1) | data formatting | bytes 131072
  28.2 0.2 copy-done
  28.5 0.6 %copy.12 = f32[4,4,8,128]{3,2,1,0:T(8,128)} copy(f32[4,4,8,128]{3,2,1,0:T(8,128)S(1)} %copy-done) | data formatting | bytes 131072
Async XLA Ops:
  26.0 1.6 %copy-start.1 = (f32[4,4,8,128]{3,2,1,0:T(8,128)S(1)}, f32[4,4,8,128]{3,2,1,0:T(8,128)}, u32[]{:S(2)}) copy-start(f32[4,4,8,128]{3,2,1,0:T(8,128)} %get-tuple-element.17) | copy-start | bytes 196612
  27.6 0.9 %copy-start = (f32[4,4,8,128]{3,2,1,0:T(8,128)S(1)}, f32[4,4,8,128]{3,2,1,0:T(8,128)}, u32[]{:S(2)}) copy-start(f32[4,4,8,128]{3,2,1,0:T(8,128)} %get-tuple-element.18) | copy-start | bytes 196612

commit v2 on v1

--- a/solution.py
+++ b/solution.py
@@ -624,9 +624,9 @@
         rate, gravity, source, norm = pl.pallas_call(
             kernel,
             out_shape=(
-                jax.ShapeDtypeStruct((5,) + shape, jnp.float32),
-                jax.ShapeDtypeStruct((4,) + shape, jnp.float32),
-                jax.ShapeDtypeStruct((4,) + shape, jnp.float32),
+                pltpu.VMEM((5,) + shape, jnp.float32),
+                pltpu.VMEM((4,) + shape, jnp.float32),
+                pltpu.VMEM((4,) + shape, jnp.float32),
                 jax.ShapeDtypeStruct((1, 1), jnp.float32),
             ),
             in_specs=[pl.BlockSpec(memory_space=pl.ANY)] * 2,

time: 31.1 us -> 29.7 us (0.955)
  local copies, waits for them, and re-layouts: 3.05 us -> 1.9 us
    unnamed x7 -> x3, local copies, waits for them, and re-layouts: 3.05 us -> 1.9 us
where the time goes in v2:
time: 29.7 us; the launch traced here: 29.5 us
  Pallas kernels  25.3 us (85%)
  between operations  2.33 us (8%)
  local copies, waits for them, and re-layouts  1.9 us (6%)
    pallas_call x1, Pallas kernels, local(): pl.pallas_call(kernel, out_shape=(pltpu.VMEM((5,) + shape, jnp.float32),...  25.3 us
    unnamed x3, local copies, waits for them, and re-layouts  1.9 us

profile of v2, /device:TPU:0, one launch (start us, length us, event | category | flops | bytes accessed | tf_op | source)
XLA Modules:
  0.0 29.5 jit_solution(11013124436270854586)
XLA Ops:
  0.6 25.3 %shard_map.57 = (f32[5,4,8,128]{3,2,1,0:T(8,128)S(1)}, f32[4,4,8,128]{3,2,1,0:T(8,128)S(1)}, f32[4,4,8,128]{3,2,1,0:T(8,128)S(1)}, f32[1,1]{1,0:T(1,128)}) custom-call(f32[5,4,8,128]{3,2,1,0:T(8,128)} %euler_hbm.1, f32[4,4,8,128]{3,2,1,0:T(8,128)} %gravity_hbm.1), custom_call_target="tpu_custom_call" | custom-call | tf_op jit(solution)/shard_map/pallas_call | solution.py:624
  25.9 0.6 %copy.10 = f32[5,4,8,128]{3,2,1,0:T(8,128)} copy(f32[5,4,8,128]{3,2,1,0:T(8,128)S(1)} %get-tuple-element.12) | data formatting | bytes 163840
  26.6 0.6 %copy.11 = f32[4,4,8,128]{3,2,1,0:T(8,128)} copy(f32[4,4,8,128]{3,2,1,0:T(8,128)S(1)} %get-tuple-element.13) | data formatting | bytes 131072
  27.2 0.6 %copy.12 = f32[4,4,8,128]{3,2,1,0:T(8,128)} copy(f32[4,4,8,128]{3,2,1,0:T(8,128)S(1)} %get-tuple-element.14) | data formatting | bytes 131072

commit v3 on v2

--- a/solution.py
+++ b/solution.py
@@ -64,10 +64,9 @@
 
 
 def reduce_stages(sizes):
+    lines = [(axis,) for axis in AXES]
     total = math.prod(sizes[axis] for axis in AXES)
-    if total <= MOST_PARTNERS:
-        return [AXES]
-    return [("gx", "gy"), ("gz",)]
+    return [lines, [AXES] if total <= MOST_PARTNERS else lines]
 
 
 def offsets_of(axes, sizes):
@@ -177,13 +176,13 @@
 def gravity_interface(left, right, direction):
     result = []
     for var in range(4):
-        jump = 0.5 * grav_speed * (right[var] - left[var])
-        if var == 0:
-            result.append(-0.5 * (left[1 + direction] + right[1 + direction]) - jump)
-        elif var == 1 + direction:
-            result.append(-(0.5 / relax_time) * (left[0] + right[0]) - jump)
-        else:
-            result.append(-jump)
+        parts = []
+        other = 1 + direction if var == 0 else 0
+        if var in (0, 1 + direction) and left[other] is not None:
+            parts.append(-(0.5 / relax_time if var else 0.5) * (left[other] + right[other]))
+        if left[var] is not None:
+            parts.append((-0.5 * grav_speed) * (right[var] - left[var]))
+        result.append(sum(parts[1:], parts[0]) if parts else None)
     return result
 
 
@@ -283,8 +282,8 @@
         reduce_send,
         *rest,
     ):
-        reduce_recv = rest[: len(stages)]
-        load_sem, send_sem, recv_sem, reduce_send_sem, reduce_recv_sem = rest[len(stages) :]
+        reduce_recv = [rest[: len(stages[0])], rest[len(stages[0]) : -5]]
+        load_sem, send_sem, recv_sem, reduce_send_sem, reduce_recv_sem = rest[-5:]
         place = {axis: lax.axis_index(axis) for axis in AXES}
 
         def moved(axis, by):
@@ -302,14 +301,16 @@
 
         barrier = pltpu.get_barrier_semaphore()
         count = 0
-        for axes in stages:
+        for axes in stages[0]:
             for offset in offsets_of(axes, sizes):
                 pl.semaphore_signal(
                     barrier, inc=1, device_id=device(axes, offset), device_id_type=MESH
                 )
                 count += 1
         load_euler = pltpu.make_async_copy(euler_hbm, euler_ref, load_sem.at[0])
-        load_gravity = pltpu.make_async_copy(gravity_hbm, grav_bufs.at[0], load_sem.at[1])
+        load_gravity = pltpu.make_async_copy(
+            gravity_hbm, grav_bufs.at[0, pl.ds(0, 4)], load_sem.at[1]
+        )
         load_euler.start()
         load_gravity.start()
         load_euler.wait()
@@ -330,8 +331,10 @@
             send_z[round_at, 0] = lanes[0]
             send_z[round_at, 1] = lanes[1]
 
-        def exchange(round_at):
+        def exchange(round_at, vars_at):
             copies = []
+            packed = (vars_at + 5 if round_at == 0 else vars_at) * nx
+            rows = 8 * ((packed + 7) // 8)
 
             def send(src, dst, slot, axis, by):
                 copy = pltpu.make_async_remote_copy(
@@ -350,9 +353,12 @@
                 if round_at == 0:
                     send(euler_ref.at[:, face], halo_xe.at[side], 6 + side, "gx", by)
                 send(
-                    grav_bufs.at[round_at, :, face], halo_xg.at[round_at, side], side, "gx", by
-                )
-                rows = recv_y.shape[2] if round_at == 0 else 8 * ((4 * nx + 7) // 8)
+                    grav_bufs.at[round_at, pl.ds(0, vars_at), face],
+                    halo_xg.at[round_at, side, pl.ds(0, vars_at)],
+                    side,
+                    "gx",
+                    by,
+                )
                 send(
                     send_y.at[round_at, side, pl.ds(0, rows)],
                     recv_y.at[round_at, side, pl.ds(0, rows)],
@@ -370,14 +376,13 @@
             return jnp.broadcast_to(column[:, at : at + 1], (ny, nz))
 
         def reduce_start(round_at, stage_at, rows):
-            axes = stages[stage_at]
+            axes = stages[round_at][stage_at]
             for at, row in enumerate(rows):
                 reduce_send[round_at, stage_at, at] = row
-            copies = []
             for slot, offset in enumerate(offsets_of(axes, sizes)):
                 copy = pltpu.make_async_remote_copy(
                     src_ref=reduce_send.at[round_at, stage_at, pl.ds(0, len(rows))],
-                    dst_ref=reduce_recv[stage_at].at[round_at, slot, pl.ds(0, len(rows))],
+                    dst_ref=reduce_recv[round_at][stage_at].at[slot],
                     send_sem=reduce_send_sem.at[round_at, stage_at],
                     recv_sem=reduce_recv_sem.at[round_at, stage_at],
                     device_id=device(axes, offset),
@@ -385,28 +390,21 @@
                 )
                 copy.start()
 
-        def reduce_finish(round_at, rows, combine):
-            for stage_at in range(len(stages)):
-                if stage_at > 0:
-                    reduce_start(round_at, stage_at, rows)
-                got = reduce_recv[stage_at].at[round_at, :, pl.ds(0, len(rows))]
-                pltpu.make_async_copy(got, got, reduce_recv_sem.at[round_at, stage_at]).wait()
-                pltpu.make_async_copy(got, got, reduce_send_sem.at[round_at, stage_at]).wait()
-                partners = reduce_recv[stage_at].shape[1]
-                new_rows = []
-                for at, row in enumerate(rows):
-                    parts = [row] + [
-                        reduce_recv[stage_at][round_at, slot, at] for slot in range(partners)
+        def reduce_step(round_at, stage_at, rows, combine):
+            got = reduce_recv[round_at][stage_at]
+            pltpu.make_async_copy(got, got, reduce_recv_sem.at[round_at, stage_at]).wait()
+            pltpu.make_async_copy(got, got, reduce_send_sem.at[round_at, stage_at]).wait()
+            new_rows = []
+            for at, row in enumerate(rows):
+                parts = [row] + [got[slot, at] for slot in range(got.shape[0])]
+                while len(parts) > 1:
+                    pairs = [
+                        combine[at](parts[item], parts[item + 1])
+                        for item in range(0, len(parts) - 1, 2)
                     ]
-                    while len(parts) > 1:
-                        pairs = [
-                            combine[at](parts[item], parts[item + 1])
-                            for item in range(0, len(parts) - 1, 2)
-                        ]
-                        parts = pairs + ([parts[-1]] if len(parts) % 2 else [])
-                    new_rows.append(parts[0])
-                rows = new_rows
-            return rows
+                    parts = pairs + ([parts[-1]] if len(parts) % 2 else [])
+                new_rows.append(parts[0])
+            return new_rows
 
         pack(0, state + grav)
         nodes = [primitive([state[var][x] for var in range(5)]) for x in range(nx)]
@@ -425,7 +423,7 @@
         first_rows = [jnp.max(fastest, axis=0, keepdims=True), weighted_row(state[0])]
 
         pl.semaphore_wait(barrier, count)
-        copies_0 = exchange(0)
+        copies_0 = exchange(0, 4)
         reduce_start(0, 0, first_rows)
 
         alpha = element_alpha(nodes, plane, nx)
@@ -435,6 +433,9 @@
 
         for copy in copies_0:
             copy.wait()
+        first_combine = [jnp.maximum, jnp.add]
+        first_rows = reduce_step(0, 0, first_rows, first_combine)
+        reduce_start(0, 1, first_rows)
 
         def face_coefs(axis, alpha_x):
             start = jnp.where(plane.is_node[axis][0], 1.0, alpha_x)
@@ -483,133 +484,175 @@
             )
             for var in range(5):
                 rate_ref[var, x] = rate[var][x]
-        mass_rows = [weighted_row(rate[0])]
-        reduce_start(1, 0, mass_rows)
-
-        first_rows = reduce_finish(0, first_rows, [jnp.maximum, jnp.add])
-        fastest = jnp.max(first_rows[0], axis=1, keepdims=True)
-        mean_now = jnp.sum(first_rows[1], axis=1, keepdims=True) * (1.0 / weight_total)
-        time_step = cfl_euler * elem_width / (7.0 * fastest)
-        state_next = [
-            [state[var][x] + time_step * rate[var][x] for x in range(nx)] for var in range(4)
-        ]
-
-        def gravity_rate(grav, round_at, offset):
-            result = [
-                [-coupling * (state_next[0][x] - offset) for x in range(nx)],
-            ] + [[-grav[1 + comp][x] / relax_time for x in range(nx)] for comp in range(3)]
+        mass_row = weighted_row(rate[0])
+
+        def gravity_rate(grav, drive):
+            result = [[-coupling * drive[x] for x in range(nx)]]
+            for comp in range(3):
+                decay = grav[1 + comp]
+                result.append(
+                    [0.0] * nx
+                    if decay[0] is None
+                    else [-decay[x] / relax_time for x in range(nx)]
+                )
             scale = -(2.0 / elem_width)
             for start in range(0, nx, 4):
                 for node in range(4):
                     for other in range(4):
                         coef = float(-scale * DERIV_FOLDED[node, other])
-                        result[0][start + node] += coef * grav[1][start + other]
+                        if grav[1][0] is not None:
+                            result[0][start + node] += coef * grav[1][start + other]
                         result[1][start + node] += coef / relax_time * grav[0][start + other]
             for axis in range(2):
                 for x in range(nx):
                     matrix = -scale * DERIV_FOLDED
-                    result[0][x] += plane.apply(matrix, grav[2 + axis][x], axis)
+                    if grav[1][0] is not None:
+                        result[0][x] += plane.apply(matrix, grav[2 + axis][x], axis)
                     result[2 + axis][x] += plane.apply(matrix / relax_time, grav[0][x], axis)
             return result, scale
 
-        def gravity_faces(result, scale, grav, round_at, first_at):
-            edges = [[halo_xg[round_at, side, var] for var in range(4)] for side in range(2)]
+        def gravity_faces(result, scale, grav, round_at, first_at, first_var):
+            live = [var for var in range(4) if grav[var][0] is not None]
+
+            def each(make):
+                return [make(var) if var in live else None for var in range(4)]
+
+            edges = [
+                each(lambda var: halo_xg[round_at, side, first_var + var]) for side in range(2)
+            ]
             row = [edges[0]] + [[grav[var][x] for var in range(4)] for x in range(nx)] + [edges[1]]
             for x in range(0, nx, 4):
                 left = gravity_interface(row[x], row[x + 1], 0)
                 right = gravity_interface(row[x + 4], row[x + 5], 0)
                 for var in range(4):
-                    result[var][x] += float(-scale / WEIGHTS[0]) * left[var]
-                    result[var][x + 3] += float(scale / WEIGHTS[3]) * right[var]
+                    if left[var] is not None:
+                        result[var][x] += float(-scale / WEIGHTS[0]) * left[var]
+                        result[var][x + 3] += float(scale / WEIGHTS[3]) * right[var]
             column = [recv_z[round_at, side] for side in range(2)]
             for axis in range(2):
                 start = plane.coef([-scale / WEIGHTS[0], 0.0, 0.0, 0.0], axis)
                 stop = plane.coef([0.0, 0.0, 0.0, scale / WEIGHTS[3]], axis)
                 for x in range(nx):
                     halos = [
-                        [
-                            halo_y(round_at, side, first_at + var * nx + x)
+                        each(
+                            lambda var: halo_y(round_at, side, first_at + var * nx + x)
                             if axis == 0
                             else halo_z(column[side], first_at + var * nx + x)
-                            for var in range(4)
-                        ]
+                        )
                         for side in range(2)
                     ]
                     here = [grav[var][x] for var in range(4)]
-                    before = [plane.previous(here[var], halos[0][var], axis) for var in range(4)]
-                    after = [plane.following(here[var], halos[1][var], axis) for var in range(4)]
+                    before = each(lambda var: plane.previous(here[var], halos[0][var], axis))
+                    after = each(lambda var: plane.following(here[var], halos[1][var], axis))
                     left = gravity_interface(before, here, axis + 1)
                     right = gravity_interface(here, after, axis + 1)
                     for var in range(4):
-                        result[var][x] += start * left[var] + stop * right[var]
+                        if left[var] is not None:
+                            result[var][x] += start * left[var] + stop * right[var]
             return result
 
-        for iteration in range(ITERS):
-            rate_grav, scale = gravity_rate(grav, iteration, mean_now)
-            if iteration > 0:
-                for copy in copies:
-                    copy.wait()
-            rate_grav = gravity_faces(
-                rate_grav, scale, grav, iteration, 5 * nx if iteration == 0 else 0
+        def step(old, change):
+            return [
+                [
+                    pseudo_step * change[var][x]
+                    if old[var][x] is None
+                    else old[var][x] + pseudo_step * change[var][x]
+                    for x in range(nx)
+                ]
+                for var in range(4)
+            ]
+
+        rate_grav, scale = gravity_rate(grav, state[0])
+        rate_grav = gravity_faces(rate_grav, scale, grav, 0, 5 * nx, 0)
+        none = [None] * nx
+        more = [[(-pseudo_step * coupling) * rate[0][x] for x in range(nx)], none, none, none]
+        for iteration in range(1, ITERS):
+            grav = step(grav, rate_grav)
+            if iteration > 1:
+                more = step(more, rate_more)
+            fields = grav + [items for items in more if items[0] is not None]
+            for var, items in enumerate(fields):
+                for x in range(nx):
+                    grav_bufs[iteration, var, x] = items[x]
+            pack(iteration, fields)
+            copies = exchange(iteration, len(fields))
+            rate_grav, scale = gravity_rate(grav, state[0])
+            rate_more, scale = gravity_rate(more, rate[0])
+            for copy in copies:
+                copy.wait()
+            if iteration < len(stages[0]):
+                first_rows = reduce_step(0, iteration, first_rows, first_combine)
+                if iteration + 1 < len(stages[0]):
+                    reduce_start(0, iteration + 1, first_rows)
+            rate_grav = gravity_faces(rate_grav, scale, grav, iteration, 0, 0)
+            rate_more = gravity_faces(rate_more, scale, more, iteration, 4 * nx, 4)
+
+        fastest = jnp.max(first_rows[0], axis=1, keepdims=True)
+        mean_now = jnp.sum(first_rows[1], axis=1, keepdims=True) * (1.0 / weight_total)
+        time_step = cfl_euler * elem_width / (7.0 * fastest)
+        rate_phi = [
+            rate_grav[0][x] + time_step * rate_more[0][x] + coupling * mean_now for x in range(nx)
+        ]
+        last_rows = [
+            weighted_row([item * item for item in rate_phi]),
+            weighted_row(rate_phi),
+            mass_row,
+        ]
+        reduce_start(1, 0, last_rows)
+        state_next = [
+            [state[var][x] + time_step * rate[var][x] for x in range(nx)] for var in range(4)
+        ]
+        earlier = ((ITERS - 1) * pseudo_step * coupling) * mean_now
+        phi = [
+            grav[0][x] + time_step * more[0][x] + (pseudo_step * rate_phi[x] + earlier)
+            for x in range(nx)
+        ]
+        grav, more = step(grav, rate_grav), step(more, rate_more)
+        for x in range(nx):
+            grad = [grav[1 + comp][x] + time_step * more[1 + comp][x] for comp in range(3)]
+            for comp in range(3):
+                grav_ref[1 + comp, x] = grad[comp]
+                source_ref[comp, x] = -state_next[0][x] * grad[comp]
+            source_ref[3, x] = -(
+                state_next[1][x] * grad[0]
+                + state_next[2][x] * grad[1]
+                + state_next[3][x] * grad[2]
             )
-            if iteration < ITERS - 1:
-                grav = [
-                    [grav[var][x] + pseudo_step * rate_grav[var][x] for x in range(nx)]
-                    for var in range(4)
-                ]
-                for var in range(4):
-                    for x in range(nx):
-                        grav_bufs[iteration + 1, var, x] = grav[var][x]
-                pack(iteration + 1, grav)
-                copies = exchange(iteration + 1)
-        mass_rows = reduce_finish(1, mass_rows, [jnp.add])
-        mean_more = time_step * (
-            jnp.sum(mass_rows[0], axis=1, keepdims=True) * (1.0 / weight_total)
-        )
-        rate_phi = [item + coupling * mean_more for item in rate_grav[0]]
-        norm_rows = [weighted_row([item * item for item in rate_phi])]
-        reduce_start(2, 0, norm_rows)
-        late = (ITERS - 1) * pseudo_step * coupling * mean_more
-        rate_grav[0] = rate_phi
-        grav = [
-            [grav[var][x] + pseudo_step * rate_grav[var][x] for x in range(nx)] for var in range(4)
-        ]
+        for stage_at in range(len(stages[1])):
+            if stage_at > 0:
+                reduce_start(1, stage_at, last_rows)
+            last_rows = reduce_step(1, stage_at, last_rows, [jnp.add] * 3)
+        squared, linear, mass = [jnp.sum(item, axis=1, keepdims=True) for item in last_rows]
+        shift = coupling * (time_step * (mass * (1.0 / weight_total)))
+        squared = squared + shift * (2.0 * linear + shift * weight_total)
+        norm_ref[...] = jnp.sqrt(squared * (1.0 / weight_total))
         for x in range(nx):
-            grav[0][x] = grav[0][x] + late
-            for var in range(4):
-                grav_ref[var, x] = grav[var][x]
-            for comp in range(3):
-                source_ref[comp, x] = -state_next[0][x] * grav[1 + comp][x]
-            source_ref[3, x] = -(
-                state_next[1][x] * grav[1][x]
-                + state_next[2][x] * grav[2][x]
-                + state_next[3][x] * grav[3][x]
-            )
-        norm_rows = reduce_finish(2, norm_rows, [jnp.add])
-        squared = jnp.sum(norm_rows[0], axis=1, keepdims=True)
-        norm_ref[...] = jnp.sqrt(squared * (1.0 / weight_total))
+            grav_ref[0, x] = phi[x] + (ITERS * pseudo_step) * shift
 
     rows_y = 8 * ((9 * nx + 7) // 8)
     plane_shape = (ny, nz)
     scratch = [
         pltpu.VMEM((5, nx) + plane_shape, jnp.float32),
-        pltpu.VMEM((ITERS, 4, nx) + plane_shape, jnp.float32),
+        pltpu.VMEM((ITERS, 8, nx) + plane_shape, jnp.float32),
         pltpu.VMEM((2, 5) + plane_shape, jnp.float32),
-        pltpu.VMEM((ITERS, 2, 4) + plane_shape, jnp.float32),
+        pltpu.VMEM((ITERS, 2, 8) + plane_shape, jnp.float32),
         pltpu.VMEM((ITERS, 2, rows_y, nz), jnp.float32),
         pltpu.VMEM((ITERS, 2, rows_y, nz), jnp.float32),
         pltpu.VMEM((ITERS, 2) + plane_shape, jnp.float32),
         pltpu.VMEM((ITERS, 2) + plane_shape, jnp.float32),
-        pltpu.VMEM((3, len(stages), 2, 1, nz), jnp.float32),
+        pltpu.VMEM((2, len(stages[0]), 3, 1, nz), jnp.float32),
     ]
-    for axes in stages:
-        scratch.append(pltpu.VMEM((3, len(offsets_of(axes, sizes)), 2, 1, nz), jnp.float32))
+    for round_at, rows in enumerate((2, 3)):
+        for axes in stages[round_at]:
+            scratch.append(
+                pltpu.VMEM((len(offsets_of(axes, sizes)), rows, 1, nz), jnp.float32)
+            )
     scratch += [
         pltpu.SemaphoreType.DMA((2,)),
         pltpu.SemaphoreType.DMA((ITERS, 8)),
         pltpu.SemaphoreType.DMA((ITERS, 8)),
-        pltpu.SemaphoreType.DMA((3, len(stages))),
-        pltpu.SemaphoreType.DMA((3, len(stages))),
+        pltpu.SemaphoreType.DMA((2, len(stages[0]))),
+        pltpu.SemaphoreType.DMA((2, len(stages[0]))),
     ]
     return kernel, scratch
 

time: 29.7 us -> 28.3 us (0.953)
  Pallas kernels: 25.3 us -> 23.9 us
    pallas_call x1, Pallas kernels: 25.3 us -> 23.9 us  [local(): pl.pallas_call(kernel, out_shape=(pltpu.VMEM((5,) + shape, jnp.float32),...]
where the time goes in v3:
time: 28.3 us; the launch traced here: 28.1 us
  Pallas kernels  23.9 us (84%)
  between operations  2.33 us (8%)
  local copies, waits for them, and re-layouts  1.9 us (7%)
    pallas_call x1, Pallas kernels, local(): pl.pallas_call(kernel, out_shape=(pltpu.VMEM((5,) + shape, jnp.float32),...  23.9 us
    unnamed x3, local copies, waits for them, and re-layouts  1.9 us

profile of v3, /device:TPU:0, one launch (start us, length us, event | category | flops | bytes accessed | tf_op | source)
XLA Modules:
  0.0 28.1 jit_solution(15762907499710790462)
XLA Ops:
  0.6 23.9 %shard_map.57 = (f32[5,4,8,128]{3,2,1,0:T(8,128)S(1)}, f32[4,4,8,128]{3,2,1,0:T(8,128)S(1)}, f32[4,4,8,128]{3,2,1,0:T(8,128)S(1)}, f32[1,1]{1,0:T(1,128)}) custom-call(f32[5,4,8,128]{3,2,1,0:T(8,128)} %euler_hbm.1, f32[4,4,8,128]{3,2,1,0:T(8,128)} %gravity_hbm.1), custom_call_target="tpu_custom_call" | custom-call | tf_op jit(solution)/shard_map/pallas_call | solution.py:667
  24.5 0.6 %copy.10 = f32[5,4,8,128]{3,2,1,0:T(8,128)} copy(f32[5,4,8,128]{3,2,1,0:T(8,128)S(1)} %get-tuple-element.12) | data formatting | bytes 163840
  25.2 0.6 %copy.11 = f32[4,4,8,128]{3,2,1,0:T(8,128)} copy(f32[4,4,8,128]{3,2,1,0:T(8,128)S(1)} %get-tuple-element.13) | data formatting | bytes 131072
  25.8 0.6 %copy.12 = f32[4,4,8,128]{3,2,1,0:T(8,128)} copy(f32[4,4,8,128]{3,2,1,0:T(8,128)S(1)} %get-tuple-element.14) | data formatting | bytes 131072

commit v4 on v3

--- a/solution.py
+++ b/solution.py
@@ -670,7 +670,7 @@
                 pltpu.VMEM((5,) + shape, jnp.float32),
                 pltpu.VMEM((4,) + shape, jnp.float32),
                 pltpu.VMEM((4,) + shape, jnp.float32),
-                jax.ShapeDtypeStruct((1, 1), jnp.float32),
+                pltpu.VMEM((1, 1), jnp.float32),
             ),
             in_specs=[pl.BlockSpec(memory_space=pl.ANY)] * 2,
             out_specs=(vmem, vmem, vmem, vmem),

time: 28.3 us -> 27.3 us (0.965)
  between operations: 2.33 us -> 1.8 us
  Pallas kernels: 23.9 us -> 23.4 us
    pallas_call x1, Pallas kernels: 23.9 us -> 23.4 us  [local(): pl.pallas_call(kernel, out_shape=(pltpu.VMEM((5,) + shape, jnp.float32),...]
where the time goes in v4:
time: 27.3 us; the launch traced here: 27.1 us
  Pallas kernels  23.4 us (86%)
  local copies, waits for them, and re-layouts  1.9 us (7%)
  between operations  1.8 us (7%)
    pallas_call x1, Pallas kernels, local(): pl.pallas_call(kernel, out_shape=(pltpu.VMEM((5,) + shape, jnp.float32),...  23.4 us
    unnamed x3, local copies, waits for them, and re-layouts  1.9 us

profile of v4, /device:TPU:0, one launch (start us, length us, event | category | flops | bytes accessed | tf_op | source)
XLA Modules:
  0.0 27.1 jit_solution(853567066395859420)
XLA Ops:
  0.6 23.4 %shard_map.57 = (f32[5,4,8,128]{3,2,1,0:T(8,128)S(1)}, f32[4,4,8,128]{3,2,1,0:T(8,128)S(1)}, f32[4,4,8,128]{3,2,1,0:T(8,128)S(1)}, f32[1,1]{1,0:T(1,128)S(1)}) custom-call(f32[5,4,8,128]{3,2,1,0:T(8,128)} %euler_hbm.1, f32[4,4,8,128]{3,2,1,0:T(8,128)} %gravity_hbm.1), custom_call_target="tpu_custom_call" | custom-call | tf_op jit(solution)/shard_map/pallas_call | solution.py:667
  24.1 0.6 %copy.10 = f32[5,4,8,128]{3,2,1,0:T(8,128)} copy(f32[5,4,8,128]{3,2,1,0:T(8,128)S(1)} %get-tuple-element.12) | data formatting | bytes 163840
  24.7 0.6 %copy.11 = f32[4,4,8,128]{3,2,1,0:T(8,128)} copy(f32[4,4,8,128]{3,2,1,0:T(8,128)S(1)} %get-tuple-element.13) | data formatting | bytes 131072
  25.3 0.6 %copy.12 = f32[4,4,8,128]{3,2,1,0:T(8,128)} copy(f32[4,4,8,128]{3,2,1,0:T(8,128)S(1)} %get-tuple-element.14) | data formatting | bytes 131072
